TPU v7x, 128 devices: a whole 4x4x4 slice. The times are simulated.
128 devices in a mesh: row: 32 (over z, x, core), sub: 4 (over y).
Axes of the slice: x: 4, y: 4, z: 4, core: 2. Of those that a mesh axis runs over, the one named last changes fastest.
Arguments:
- eig_vectors: float32 [262144, 512], P(('row', 'sub')), may hold values from -0.01171875 to 0.01171875
- vec_cotangent: float32 [262144, 512], P(('row', 'sub')), may hold values from -3072 to 3072
- levels: float32 [512], replicated, may hold values from -2 to 2
- order: int32 [512], replicated, may hold values from 0 to 511, each once
- neighbours: int32 [2048, 12], P(('row', 'sub')), may hold values from 0 to 2047, as said below
Outputs:
- grad_blocks: float32 [2048, 12, 128, 128], P(('row', 'sub'))
Inputs may be any that keep to these rules, and one draw needn't show every extreme that they name: `neighbours`: entry 0 of row i is i itself. Row blocks are dealt to devices in order, 16 to a device, device index = row index * 4 + sub index; every listed block lies on the row block's own device or on a device whose row index or sub index (not both) differs by one, cyclically.
All inputs are finite; a program needn't handle non-finite values.
Results may differ from a plain program's by a relative error of at most 0.0003.
Values sent between devices are 32-bit elements; how exact they have to be, the bound alone decides.
No kernel may reach another device: no remote copies, remote signals or barrier semaphores. Data moves between devices by JAX's collectives and lax.ppermute only.
A program may use at most 192 MiB of HBM per device.

v0:
```python
import jax
import jax.numpy as jnp
from jax import lax
from jax.sharding import PartitionSpec as P

BS = 128


broadening_sq = 0.0025


def with_halo(block, sides, width):
    for axis, dim in sides:
        count = lax.axis_size(axis)
        forward = [(i, i + 1) for i in range(count - 1)]
        forward.append((count - 1, 0))
        backward = [(target, source) for source, target in forward]
        low = lax.ppermute(
            lax.slice_in_dim(block, block.shape[dim] - width, None, axis=dim), axis, forward
        )
        high = lax.ppermute(lax.slice_in_dim(block, 0, width, axis=dim), axis, backward)
        block = jnp.concatenate([low, block, high], axis=dim)
    return block


def gap_rows(energy, row_energy):
    spread = energy[None, :] - row_energy[:, None]
    return spread / (spread * spread + broadening_sq)


def body(eig_vectors, vec_cotangent, levels, order, neighbours):
    highest = lax.Precision.HIGHEST
    window = eig_vectors.shape[1]
    local_rows = eig_vectors.shape[0]
    blk_count = local_rows // BS
    partial_value = lax.dot_general(
        eig_vectors,
        vec_cotangent,
        (((0,), (0,)), ((), ())),
        precision=highest,
        preferred_element_type=jnp.float32,
    )
    columns = lax.broadcasted_iota(jnp.int32, (window, window), 1)
    picker = (order[:, None] == columns).astype(jnp.float32)
    energy = jnp.dot(picker, levels, precision=highest, preferred_element_type=jnp.float32)
    gram = lax.psum(partial_value, ("row", "sub"))
    scaled = gap_rows(energy, energy) * gram
    adjoint_rows = jnp.dot(
        eig_vectors, scaled, precision=highest, preferred_element_type=jnp.float32
    )
    padded = with_halo(eig_vectors.reshape(1, 1, local_rows, window), (("row", 0), ("sub", 1)), 1)
    lookup_table = padded.reshape(9 * blk_count, BS, window)
    n_row = lax.axis_size("row")
    n_sub = lax.axis_size("sub")
    my_row = lax.axis_index("row")
    my_sub = lax.axis_index("sub")
    device = neighbours // blk_count
    local = neighbours % blk_count
    row_delta = (device // n_sub - my_row + n_row) % n_row
    sub_delta = (device % n_sub - my_sub + n_sub) % n_sub
    row_slot = 1 + (row_delta == 1).astype(jnp.int32) - (row_delta == n_row - 1).astype(jnp.int32)
    sub_slot = 1 + (sub_delta == 1).astype(jnp.int32) - (sub_delta == n_sub - 1).astype(jnp.int32)
    flat_index = (row_slot * 3 + sub_slot) * blk_count + local
    adj_blocks = adjoint_rows.reshape(blk_count, BS, window)

    def one_block(inputs_pair):
        adj_block, listed = inputs_pair
        picked = jnp.take(lookup_table, listed, axis=0)
        return jnp.einsum("ak,nbk->nab", adj_block, picked, precision=highest)

    return lax.map(one_block, (adj_blocks, flat_index))


def solution(mesh):
    in_specs = (P(("row", "sub"), None), P(("row", "sub"), None), P(), P(), P(("row", "sub"), None))
    out_specs = P(("row", "sub"), None, None, None)
    return jax.shard_map(body, mesh=mesh, in_specs=in_specs, out_specs=out_specs, check_vma=False)
```

profile of v0, /device:TPU:24, one launch (start us, length us, event | category | flops | bytes accessed | tf_op | source)
XLA Modules:
  0.0 530.5 jit_solution(11525937342492526533)
XLA Ops:
  6.6 5.7 %collective-permute-start.1 = (f32[1,1,2048,512]{3,2,1,0:T(8,128)}, f32[1,1,2048,512]{3,2,1,0:T(8,128)S(1)}, u32[]{:S(2)}, u32[]{:S(2)}) collective-permute-start(f32[1,1,2048,512]{3,2,1,0:T(8,128)} %bitcast.38), channel_id=1, source_target_pairs={{4,0},{8,4},{12,8},{16,12},{20,16},{24,20},{28,24},{32,28},{36,32}... | collective-permute-start | bytes 12582920 | tf_op jit(solution)/shard_map/ppermute | solution.py:21
  12.4 46.3 %collective-permute-done = f32[1,1,2048,512]{3,2,1,0:T(8,128)S(1)} collective-permute-done((f32[1,1,2048,512]{3,2,1,0:T(8,128)}, f32[1,1,2048,512]{3,2,1,0:T(8,128)S(1)}, u32[]{:S(2)}, u32[]{:S(2)}) %collective-permute-start) | collective-permute-done | bytes 4194336 | tf_op jit(solution)/shard_map/ppermute | solution.py:18
  58.7 8.0 %pad_maximum_fusion.1 = f32[3,1,2048,512]{3,2,1,0:T(8,128)} fusion(f32[1,1,2048,512]{3,2,1,0:T(8,128)S(1)} %collective-permute-done.1, f32[1,1,2048,512]{3,2,1,0:T(8,128)} %bitcast.39, f32[1,1,2048,512]{3,2,1,0:T(8,128)S(1)} %collective-permute-done), kind=kLoop, calls=%fused_computation.18 | loop fusion | flops 6291456 | bytes 25165824 | tf_op jit(solution)/shard_map/concatenate | solution.py:22
  68.9 8.1 %fusion.30 = f32[512,512]{1,0:T(8,128)} fusion(f32[2048,512]{1,0:T(8,128)S(1)} %copy-done.2, f32[2048,512]{1,0:T(8,128)S(1)} %copy-done.5), kind=kOutput, calls=%fused_computation.58 | convolution fusion | flops 6442450944 | bytes 9437184 | tf_op jit(solution)/shard_map/dot_general | solution.py:36
  77.7 149.6 %all-reduce.2.cloned.1.call-done = f32[512,512]{1,0:T(8,128)} async-done(((f32[512,512]{1,0:T(8,128)}), f32[512,512]{1,0:T(8,128)}) %all-reduce.2.cloned.1.call-update) | async-done | bytes 1048592 | tf_op jit(solution)/shard_map/psum | solution.py:46
  227.3 16.9 %convolution_bitcast_fusion = f32[2048,512]{0,1:T(8,128)} fusion(f32[2048,512]{1,0:T(8,128)} %param.7, f32[512,512]{1,0:T(8,128)} %all-reduce.2.cloned.1.call-done, f32[512]{0:T(512)S(1)} %bitcast.42), kind=kOutput, calls=%fused_computation.19 | convolution fusion | flops 6443761664 | bytes 9439232 | tf_op jit(solution)/shard_map/dot_general | solution.py:48
  244.2 5.3 %copy.8 = f32[2048,512]{1,0:T(8,128)} copy(f32[2048,512]{0,1:T(8,128)} %convolution_bitcast_fusion) | data formatting | bytes 8388608 | tf_op jit(solution)/shard_map/while | solution.py:71
  249.5 92.8 %collective-permute-done.2 = f32[3,1,2048,512]{3,2,1,0:T(8,128)} collective-permute-done((f32[3,1,2048,512]{3,2,1,0:T(8,128)}, f32[3,1,2048,512]{3,2,1,0:T(8,128)}, u32[]{:S(2)}, u32[]{:S(2)}) %collective-permute-start.2) | collective-permute-done | bytes 12582944 | tf_op jit(solution)/shard_map/ppermute | solution.py:18
  343.8 28.2 %pad_maximum_fusion = f32[3,3,2048,512]{3,2,1,0:T(8,128)} fusion(f32[3,1,2048,512]{3,2,1,0:T(8,128)} %collective-permute-done.3, f32[1,1,2048,512]{3,2,1,0:T(8,128)} %copy-done.4, f32[1,1,2048,512]{3,2,1,0:T(8,128)} %bitcast.40, f32[1,1,2048,512]{3,2,1,0:T(8,128)} %copy-done.3, f32[3,1,2048,512]{3,2,1,0:T(8,128)} %collective-permute-done.2), kind=kLoop, calls=%fused_computation.17 | loop fusion | flops 37748736 | bytes 75497472 | tf_op jit(solution)/shard_map/concatenate | solution.py:22
  372.0 151.0 %while.10 = (s32[]{:T(128)}, f32[16,12,128,128]{3,2,1,0:T(8,128)}, s32[16,12]{1,0:T(8,128)S(1)}, f32[144,128,512]{2,1,0:T(8,128)}, f32[16,128,512]{2,1,0:T(8,128)}, /*index=5*/s32[]{:T(128)}) while((s32[]{:T(128)}, f32[16,12,128,128]{3,2,1,0:T(8,128)}, s32[16,12]{1,0:T(8,128)S(1)}, f32[144,128,512]{2,1,0:T(8,128)}, f32[16,128,512]{2,1,0:T(8,128)}, ...), condition=%wide.region_2.3_spmd, body=%wide.region_1.2_spmd.sunk | while | flops 1208747136 | bytes 13636949 | solution.py:71
  372.0 2.6 gather_fusion
  374.6 4.5 fusion.42
  381.4 2.6 gather_fusion
  384.0 4.5 fusion.42
  390.9 2.6 gather_fusion
  393.4 4.5 fusion.42
  400.3 2.6 gather_fusion
  402.9 4.5 fusion.42
  409.7 2.6 gather_fusion
  412.3 4.5 fusion.42
  421.7 4.5 fusion.42
  431.2 4.5 fusion.42
  440.6 4.5 fusion.42
  450.0 4.5 fusion.42
  459.5 4.5 fusion.42
  468.9 4.5 fusion.42
  478.3 4.5 fusion.42
  487.8 4.5 fusion.42
  497.2 4.5 fusion.42
  504.0 2.6 gather_fusion
  506.7 4.5 fusion.42
  516.1 4.5 fusion.42
  (116 shorter events, 68.6 us)
Async XLA Ops:
  6.5 70.4 %copy-start = (f32[512]{0:T(512)S(1)}, f32[512]{0:T(512)}, u32[]{:S(2)}) copy-start(f32[512]{0:T(512)} %param.9) | copy-start | bytes 6148
  6.5 220.7 %all-reduce.2.cloned.1.call-start = ((), (), s32[]{:S(2)}) async-start(), calls=%async_computation | async-start | bytes 2097152 | tf_op jit(solution)/shard_map/psum | solution.py:46
  6.5 62.3 %copy-start.2 = (f32[2048,512]{1,0:T(8,128)S(1)}, f32[2048,512]{1,0:T(8,128)}, u32[]{:S(2)}) copy-start(f32[2048,512]{1,0:T(8,128)} %param.7) | copy-start | bytes 12582916
  6.5 62.3 %copy-start.5 = (f32[2048,512]{1,0:T(8,128)S(1)}, f32[2048,512]{1,0:T(8,128)}, u32[]{:S(2)}) copy-start(f32[2048,512]{1,0:T(8,128)} %param.8) | copy-start | bytes 12582916
  6.5 52.1 %collective-permute-start = (f32[1,1,2048,512]{3,2,1,0:T(8,128)}, f32[1,1,2048,512]{3,2,1,0:T(8,128)S(1)}, u32[]{:S(2)}, u32[]{:S(2)}) collective-permute-start(f32[1,1,2048,512]{3,2,1,0:T(8,128)} %bitcast.37), channel_id=1, source_target_pairs={{0,4},{4,8},{8,12},{12,16},{16,20},{20,24},{24,28},{28,32},{32,36}... | collective-permute-start | bytes 12582920 | tf_op jit(solution)/shard_map/ppermute | solution.py:18
  6.6 52.1 %collective-permute-start.1 = (f32[1,1,2048,512]{3,2,1,0:T(8,128)}, f32[1,1,2048,512]{3,2,1,0:T(8,128)S(1)}, u32[]{:S(2)}, u32[]{:S(2)}) collective-permute-start(f32[1,1,2048,512]{3,2,1,0:T(8,128)} %bitcast.38), channel_id=1, source_target_pairs={{4,0},{8,4},{12,8},{16,12},{20,16},{24,20},{28,24},{32,28},{36,32}... | collective-permute-start | bytes 12582920 | tf_op jit(solution)/shard_map/ppermute | solution.py:21
  58.7 8.1 %copy-start.3 = (f32[1,1,2048,512]{3,2,1,0:T(8,128)}, f32[1,1,2048,512]{3,2,1,0:T(8,128)S(1)}, u32[]{:S(2)}) copy-start(f32[1,1,2048,512]{3,2,1,0:T(8,128)S(1)} %collective-permute-done) | copy-start | bytes 12582916
  58.7 8.0 %copy-start.4 = (f32[1,1,2048,512]{3,2,1,0:T(8,128)}, f32[1,1,2048,512]{3,2,1,0:T(8,128)S(1)}, u32[]{:S(2)}) copy-start(f32[1,1,2048,512]{3,2,1,0:T(8,128)S(1)} %collective-permute-done.1) | copy-start | bytes 12582916
  66.8 10.2 %copy-start.7 = (s32[512]{0:T(512)S(1)}, s32[512]{0:T(512)}, u32[]{:S(2)}) copy-start(s32[512]{0:T(512)} %param.10) | copy-start | bytes 6148
  66.8 10.9 %copy-start.6 = (s32[16,12]{1,0:T(8,128)S(1)}, s32[16,12]{1,0:T(8,128)}, u32[]{:S(2)}) copy-start(s32[16,12]{1,0:T(8,128)} %param.11) | copy-start | bytes 2308
  66.8 275.5 %collective-permute-start.2 = (f32[3,1,2048,512]{3,2,1,0:T(8,128)}, f32[3,1,2048,512]{3,2,1,0:T(8,128)}, u32[]{:S(2)}, u32[]{:S(2)}) collective-permute-start(f32[3,1,2048,512]{3,2,1,0:T(8,128)} %pad_maximum_fusion.1), channel_id=1, source_target_pairs={{0,1},{1,2},{2,3},{3,0},{4,5},{5,6},{6,7},{7,4},{8,9},{9,10},{10,1... | collective-permute-start | bytes 37748744 | tf_op jit(solution)/shard_map/ppermute | solution.py:18
  67.1 276.7 %collective-permute-start.3 = (f32[3,1,2048,512]{3,2,1,0:T(8,128)}, f32[3,1,2048,512]{3,2,1,0:T(8,128)}, u32[]{:S(2)}, u32[]{:S(2)}) collective-permute-start(f32[3,1,2048,512]{3,2,1,0:T(8,128)} %pad_maximum_fusion.1), channel_id=1, source_target_pairs={{1,0},{2,1},{3,2},{0,3},{5,4},{6,5},{7,6},{4,7},{9,8},{10,9},{11,1... | collective-permute-start | bytes 37748744 | tf_op jit(solution)/shard_map/ppermute | solution.py:21
  522.9 0.7 copy-start.1
Sparse Core Ops, SparseCore 0:
  77.1 150.1 all-reduce.1
where the time goes:
time: 532 us; the launch traced here: 530 us
  waiting for transfers between devices  290 us (55%)
  matrix products  97.3 us (18%)
  local copies, waits for them, and re-layouts  84.4 us (16%)
  other arithmetic  36.8 us (7%)
  between operations  13.5 us (3%)
  starting transfers between devices  7.91 us (1%)
    psum x1, waiting for transfers between devices, body(): gram = lax.psum(partial_value, ('row', 'sub'))  150 us
    ppermute x2, waiting for transfers between devices, with_halo(): lax.ppermute(lax.slice_in_dim(block, block.shape[dim] - width, None, axis...  139 us
    dot_general x16, matrix products, one_block(): return jnp.einsum('ak,nbk->nab', adj_block, picked, precision=highest)  71.8 us
    gather x16, local copies, waits for them, and re-layouts, one_block(): picked = jnp.take(lookup_table, listed, axis=0)  41.1 us
    dynamic_update_slice x32, local copies, waits for them, and re-layouts, body(): return lax.map(one_block, (adj_blocks, flat_index))  37.3 us
    concatenate x2, other arithmetic, with_halo(): block = jnp.concatenate([low, block, high], axis=dim)  36.2 us
    dot_general x1, matrix products, body(): jnp.dot(eig_vectors, scaled, precision=highest, preferred_element_type=jn...  16.9 us
  transfers between devices with their start and end apart: 5, of which 4 were waited for; matrix products, arithmetic and copies ran while one was open for 6% of the time, Pallas kernels for 0%

commit v1 on v0

v1 whole, which is shorter than its diff:
```python
import functools

import jax
import jax.numpy as jnp
from jax import lax
from jax.experimental import pallas as pl
from jax.experimental.pallas import tpu as pltpu
from jax.sharding import PartitionSpec as P


BS = 128
broadening_sq = 0.0025

N_CORE, N_X, N_Z = 2, 4, 4
N_ROW, N_SUB = N_CORE * N_X * N_Z, 4

PIECES = (6, 7, 3)
STAGES, UNROLL, FETCH, STEP = 8, 8, 6, 4
WHOLE_VMEM = 62 * 2**20
SELF, NEAR, FAR, SUB_LOW, SUB_HIGH = range(5)


def row_shift(dz, dx):
    pairs = []
    for r in range(N_ROW):
        core, x, z = r % N_CORE, (r // N_CORE) % N_X, r // (N_CORE * N_X)
        target = (((z + dz) % N_Z) * N_X + (x + dx) % N_X) * N_CORE + core
        pairs.append((r, target))
    return pairs


CORE_SWAP = [(r, r ^ 1) for r in range(N_ROW)]


PASS_ON = [(r, (r + (-2 if r % 2 else 2)) % N_ROW) for r in range(N_ROW)]


def ring(count, step):
    return [(i, (i + step) % count) for i in range(count)]


def part(array, index, size):
    return lax.dynamic_slice_in_dim(array, index * size, size, axis=0)


def gather_back(mine, count, send):
    return jnp.concatenate([mine] + [send(step) for step in range(1, count)])


def split(value):
    high = value.astype(jnp.bfloat16)
    return high, (value - high.astype(jnp.float32)).astype(jnp.bfloat16)


def turn_kernel(blocks, out, held, turned, sems, out_sems):
    count = out.shape[0]
    fetch = [pltpu.make_async_copy(blocks.at[b], held.at[b], sems.at[b]) for b in range(count)]
    store = [pltpu.make_async_copy(turned.at[b], out.at[b], out_sems.at[b]) for b in range(count)]
    for b in range(count):
        fetch[b].start()
    for b in range(count):
        fetch[b].wait()
        turned[b] = held[b].T
        store[b].start()
    for b in range(count):
        store[b].wait()


def turn(blocks, count):
    _, rows, window = blocks.shape
    return pl.pallas_call(
        turn_kernel,
        out_shape=jax.ShapeDtypeStruct((count, window, rows), jnp.float32),
        in_specs=[pl.BlockSpec(memory_space=pltpu.HBM)],
        out_specs=pl.BlockSpec(memory_space=pltpu.HBM),
        scratch_shapes=[
            pltpu.VMEM((count, rows, window), jnp.float32),
            pltpu.VMEM((count, window, rows), jnp.float32),
            pltpu.SemaphoreType.DMA((count,)),
            pltpu.SemaphoreType.DMA((count,)),
        ],
        compiler_params=pltpu.CompilerParams(vmem_limit_bytes=WHOLE_VMEM),
        cost_estimate=pl.CostEstimate(
            flops=10**9, bytes_accessed=2 * count * rows * window * 4, transcendentals=0
        ),
        name="turn",
    )(blocks)


def front_kernel(spans, blocks, other, *refs):
    n_out = len(spans)
    outs = refs[:n_out]
    divided, gram, q, v, turned, halves, q_sems, v_sems, t_sems, d_sems = refs[n_out:]
    count = blocks.shape[0]

    def fetch(b):
        return (
            pltpu.make_async_copy(blocks.at[b], q.at[b], q_sems.at[b]),
            pltpu.make_async_copy(other.at[b], v.at[b], v_sems.at[b]),
        )

    def keep(b):
        return pltpu.make_async_copy(halves.at[b], divided.at[b], d_sems.at[b])

    def store(b, low, out):
        return pltpu.make_async_copy(turned.at[b], out.at[b - low], t_sems.at[b])

    for b in range(count):
        for copy in fetch(b):
            copy.start()
    gram[...] = jnp.zeros_like(gram)

    def step(n, _):
        left, right = [], []
        for u in range(STEP):
            b = n * STEP + u
            for copy in fetch(b):
                copy.wait()
            t = q[b].T
            turned[b] = t
            high, low = split(t)
            halves[b, :, :BS] = high
            halves[b, :, BS:] = low
            keep(b).start()
            for (first, last), out in zip(spans, outs):

                @pl.when((b >= first) & (b < last))
                def _(first=first, out=out):
                    store(b, first, out).start()

            vh, vl = split(v[b])
            left += [high, high, low]
            right += [vh, vl, vh]
        gram[...] += jnp.dot(
            jnp.concatenate(left, axis=1),
            jnp.concatenate(right, axis=0),
            preferred_element_type=jnp.float32,
        )
        return 0

    lax.fori_loop(0, count // STEP, step, 0)
    for b in range(count):
        keep(b).wait()
        for (first, last), out in zip(spans, outs):
            if first <= b < last:
                store(b, first, out).wait()


def front(blocks, other, spans):
    count, rows, window = blocks.shape
    hbm = pl.BlockSpec(memory_space=pltpu.HBM)
    return pl.pallas_call(
        functools.partial(front_kernel, spans),
        out_shape=[
            jax.ShapeDtypeStruct((high - low, window, rows), jnp.float32) for low, high in spans
        ]
        + [
            jax.ShapeDtypeStruct((count, window, 2 * rows), jnp.bfloat16),
            jax.ShapeDtypeStruct((window, window), jnp.float32),
        ],
        in_specs=[hbm, hbm],
        out_specs=[hbm] * (len(spans) + 1) + [pl.BlockSpec(memory_space=pltpu.VMEM)],
        scratch_shapes=[
            pltpu.VMEM((count, rows, window), jnp.float32),
            pltpu.VMEM((count, rows, window), jnp.float32),
            pltpu.VMEM((count, window, rows), jnp.float32),
            pltpu.VMEM((count, window, 2 * rows), jnp.bfloat16),
        ]
        + [pltpu.SemaphoreType.DMA((count,))] * 4,
        compiler_params=pltpu.CompilerParams(vmem_limit_bytes=WHOLE_VMEM),
        cost_estimate=pl.CostEstimate(
            flops=6 * count * rows * window * window, bytes_accessed=2**24, transcendentals=0
        ),
        name="front",
    )(blocks, other)


def adjoint_kernel(place, blocks, mine, other, factor, out, q, sh, sl, sems):
    count = blocks.shape[0]
    half = mine.shape[0]
    copies = [pltpu.make_async_copy(blocks.at[b], q.at[b], sems.at[b]) for b in range(count)]
    for copy in copies:
        copy.start()
    core, x, z = place[0], place[1], place[2]
    size = half // (N_X * N_Z)
    for index, ref in enumerate((mine, other)):
        start = jnp.where(core == index, 0, half)
        for i in range(N_X):
            for j in range(N_Z):
                at = start + (lax.rem(x + N_X - i, N_X) * N_Z + lax.rem(z + N_Z - j, N_Z)) * size
                rows = pl.ds(pl.multiple_of(at, size), size)
                part_of = ref[(i * N_Z + j) * size : (i * N_Z + j + 1) * size, :]
                sh[rows, :], sl[rows, :] = split(factor[rows, :] * part_of)

    def some(n, _):
        for u in range(STEP):
            i = n * STEP + u
            pltpu.make_async_copy(blocks.at[i], q.at[i], sems.at[i]).wait()
            qh, ql = split(q[i])
            both = jnp.concatenate([qh, ql], axis=0)
            first = jnp.dot(both, sh[...], preferred_element_type=jnp.float32)
            second = jnp.dot(qh, sl[...], preferred_element_type=jnp.float32)
            high, low = split(first[:BS] + (first[BS:] + second))
            out[i, :BS, :] = high
            out[i, BS:, :] = low
        return 0

    lax.fori_loop(0, count // STEP, some, 0)


def adjoint(place, blocks, mine, other, factor):
    count, rows, window = blocks.shape
    vmem = pl.BlockSpec(memory_space=pltpu.VMEM)
    return pl.pallas_call(
        adjoint_kernel,
        out_shape=jax.ShapeDtypeStruct((count, 2 * rows, window), jnp.bfloat16),
        in_specs=[pl.BlockSpec(memory_space=pltpu.SMEM), pl.BlockSpec(memory_space=pltpu.HBM)]
        + [vmem] * 3,
        out_specs=vmem,
        scratch_shapes=[
            pltpu.VMEM((count, rows, window), jnp.float32),
            pltpu.VMEM((window, window), jnp.bfloat16),
            pltpu.VMEM((window, window), jnp.bfloat16),
            pltpu.SemaphoreType.DMA((count,)),
        ],
        compiler_params=pltpu.CompilerParams(vmem_limit_bytes=WHOLE_VMEM),
        cost_estimate=pl.CostEstimate(
            flops=6 * count * rows * window * window, bytes_accessed=2**23, transcendentals=0
        ),
        name="adjoint",
    )(place, blocks, mine, other, factor)


def pair_kernel(counts, own, group, bounds, keys, adjoint_blocks, *refs):
    n_src = len(counts)
    sources = refs[:n_src]
    out, held, adjoints, fetched, stage, sems, fetch_sems, own_sem, adjoint_sem = refs[-9:]
    base = own
    pieces = [(source, b) for source, count in zip(sources, counts) for b in range(count)]
    copies = [
        pltpu.make_async_copy(source.at[b], fetched.at[n % FETCH], fetch_sems.at[n % FETCH])
        for n, (source, b) in enumerate(pieces)
    ]
    for copy in copies[:FETCH]:
        copy.start()
    adjoint_copy = pltpu.make_async_copy(adjoint_blocks, adjoints, adjoint_sem)
    adjoint_copy.start()
    if own:
        own_copy = pltpu.make_async_copy(refs[n_src], held.at[pl.ds(0, own)], own_sem)
        own_copy.start()
    for n, copy in enumerate(copies):
        copy.wait()
        high, low = split(fetched[n % FETCH])
        held[base + n, :, :BS] = high
        held[base + n, :, BS:] = low
        if n + FETCH < len(copies):
            copies[n + FETCH].start()
    adjoint_copy.wait()
    if own:
        own_copy.wait()
    first, last = bounds[group], bounds[group + 1]
    origin = bounds[group + 8]
    total = last - first

    def copy_out(slot, target):
        return pltpu.make_async_copy(stage.at[slot], out.at[target], sems.at[slot])

    def some(step, _):
        products, targets = [], []
        for u in range(UNROLL):
            key = keys[jnp.minimum(first + step * UNROLL + u, last - 1)]
            b, i, k = (key >> 8) - origin, (key >> 4) & 15, key & 15
            product = jnp.dot(adjoints[i], held[b], preferred_element_type=jnp.float32)
            products.append(
                product[:BS, :BS]
                + ((product[:BS, BS:] + product[BS:, :BS]) + product[BS:, BS:])
            )
            targets.append(i * 12 + k)
        for u in range(UNROLL):
            at = step * UNROLL + u
            slot = lax.rem(at, STAGES)

            @pl.when((at >= STAGES) & (at - STAGES < total))
            def _():
                copy_out(slot, 0).wait()

            stage[slot] = products[u]

            @pl.when(at < total)
            def _():
                copy_out(slot, targets[u]).start()

        return 0

    steps = lax.div(total + (UNROLL - 1), UNROLL)
    lax.fori_loop(0, steps, some, 0)
    done = steps * UNROLL
    for s in range(STAGES):
        at = done - STAGES + s

        @pl.when((at >= 0) & (at < total))
        def _():
            copy_out(lax.rem(at, STAGES), 0).wait()


def pair_call(group, bounds, keys, adjoints, sources, own, out, shape):
    counts = tuple(s.shape[0] for s in sources)
    n_own = 0 if own is None else own.shape[0]
    n_blk = sum(counts) + n_own
    smem = pl.BlockSpec(memory_space=pltpu.SMEM)
    hbm = pl.BlockSpec(memory_space=pltpu.HBM)
    window = adjoints.shape[-1]
    operands = [bounds, keys, adjoints, *sources]
    if own is not None:
        operands.append(own)
    aliases = {}
    if out is not None:
        aliases = {len(operands): 0}
        operands.append(out)
    return pl.pallas_call(
        functools.partial(pair_kernel, counts, n_own, group),
        out_shape=jax.ShapeDtypeStruct(shape, jnp.float32),
        in_specs=[smem, smem] + [hbm] * (len(operands) - 2),
        out_specs=hbm,
        scratch_shapes=[
            pltpu.VMEM((n_blk, window, 2 * BS), jnp.bfloat16),
            pltpu.VMEM(adjoints.shape, jnp.bfloat16),
            pltpu.VMEM((FETCH, window, BS), jnp.float32),
            pltpu.VMEM((STAGES, BS, BS), jnp.float32),
            pltpu.SemaphoreType.DMA((STAGES,)),
            pltpu.SemaphoreType.DMA((FETCH,)),
            pltpu.SemaphoreType.DMA,
            pltpu.SemaphoreType.DMA,
        ],
        input_output_aliases=aliases,
        compiler_params=pltpu.CompilerParams(vmem_limit_bytes=WHOLE_VMEM),
        cost_estimate=pl.CostEstimate(
            flops=n_blk * 4 * 2 * BS * BS * window, bytes_accessed=8 * 2**20, transcendentals=0
        ),
    )(*operands)


def body(eig_vectors, vec_cotangent, levels, order, neighbours):
    highest = lax.Precision.HIGHEST
    window = eig_vectors.shape[1]
    local_rows = eig_vectors.shape[0]
    blk_count = local_rows // BS
    n_nbr = neighbours.shape[1]
    my_row, my_sub = lax.axis_index("row"), lax.axis_index("sub")
    core, x, z = my_row % N_CORE, (my_row // N_CORE) % N_X, my_row // (N_CORE * N_X)
    blocks = eig_vectors.reshape(blk_count, BS, window)

    spans = [(sum(PIECES[:n]), sum(PIECES[: n + 1])) for n in range(len(PIECES))]
    turned = [turn(blocks, PIECES[0])]
    *rest, divided, partial_gram = front(
        blocks, vec_cotangent.reshape(blk_count, BS, window), spans[1:]
    )
    turned += rest
    sub_low = [lax.ppermute(t, "sub", ring(N_SUB, 1)) for t in turned]
    sub_high = [lax.ppermute(t, "sub", ring(N_SUB, -1)) for t in turned]
    near = [lax.ppermute(t, "row", CORE_SWAP) for t in turned]
    far = [lax.ppermute(t, "row", PASS_ON) for t in near]

    half = window // N_CORE
    total = part(partial_gram, core, half) + lax.ppermute(
        part(partial_gram, 1 - core, half), "row", CORE_SWAP
    )
    quarter = half // N_X
    mine = part(total, x, quarter)
    for s in range(1, N_X):
        mine += lax.ppermute(part(total, (x + s) % N_X, quarter), "row", row_shift(0, s))
    piece = quarter // N_Z
    total = mine
    mine = part(total, z, piece)
    for s in range(1, N_Z):
        mine += lax.ppermute(part(total, (z + s) % N_Z, piece), "row", row_shift(s, 0))
    total = mine
    for s in range(1, N_SUB):
        total += lax.ppermute(mine, "sub", ring(N_SUB, s))
    total = gather_back(total, N_Z, lambda s: lax.ppermute(total, "row", row_shift(s, 0)))
    total = gather_back(total, N_X, lambda s: lax.ppermute(total, "row", row_shift(0, s)))
    other = lax.ppermute(total, "row", CORE_SWAP)
    columns = lax.broadcasted_iota(jnp.int32, (window, window), 1)
    picked = (order[:, None] == columns).astype(jnp.float32)
    energy = jnp.dot(picked, levels, precision=highest, preferred_element_type=jnp.float32)
    spread = energy[None, :] - energy[:, None]
    factor = spread / (spread * spread + broadening_sq)
    place = jnp.stack([core, x, z]).astype(jnp.int32)

    device = neighbours // blk_count
    local = neighbours % blk_count
    row_delta = (device // N_SUB - my_row + N_ROW) % N_ROW
    sub_delta = (device % N_SUB - my_sub + N_SUB) % N_SUB
    slot = jnp.where(sub_delta == 1, SUB_HIGH, jnp.where(sub_delta == N_SUB - 1, SUB_LOW, SELF))
    slot = jnp.where(row_delta == jnp.where(core == 0, 1, N_ROW - 1), NEAR, slot)
    slot = jnp.where(row_delta == jnp.where(core == 0, N_ROW - 1, 1), FAR, slot)
    near = [(NEAR, low, array) for (low, _), array in zip(spans, near)]
    far = [(FAR, low, array) for (low, _), array in zip(spans, far)]
    sub = [
        [(SUB_LOW, low, below), (SUB_HIGH, low, above)]
        for (low, _), below, above in zip(spans, sub_low, sub_high)
    ]
    groups = [
        [(SELF, 0, divided)] + near + [far[0]] + sub[0],
        far[1:] + sub[1],
        sub[2],
    ]
    position = jnp.zeros_like(slot)
    base, origins = 0, []
    for group in groups:
        origins.append(base)
        for which, low, array in group:
            inside = (slot == which) & (local >= low) & (local < low + array.shape[0])
            position = jnp.where(inside, base + local - low, position)
            base += array.shape[0]
    i_index = lax.broadcasted_iota(jnp.int32, position.shape, 0)
    k_index = lax.broadcasted_iota(jnp.int32, position.shape, 1)
    key = (position * 256 + i_index * 16 + k_index).reshape(-1)
    rank = jnp.sum((key[:, None] > key[None, :]).astype(jnp.int32), axis=1)
    n_pair = key.shape[0]
    places = lax.broadcasted_iota(jnp.int32, (n_pair, n_pair), 0)
    keys = jnp.sum(jnp.where(rank[None, :] == places, key[None, :], 0), axis=1)
    limits = jnp.array(origins + [base] * (8 - len(origins)), jnp.int32)
    starts = jnp.sum((position.reshape(1, -1) < limits[:, None]).astype(jnp.int32), axis=1)
    bounds = jnp.concatenate([starts, limits])

    adjoints = adjoint(place, blocks, total, other, factor)
    out = None
    shape = (blk_count * n_nbr, BS, BS)
    for index, group in enumerate(groups):
        arrays = [g[2] for g in group]
        own = arrays.pop(0) if index == 0 else None
        out = pair_call(index, bounds, keys, adjoints, arrays, own, out, shape)
    return out.reshape(blk_count, n_nbr, BS, BS)


def solution(mesh):
    in_specs = (P(("row", "sub"), None), P(("row", "sub"), None), P(), P(), P(("row", "sub"), None))
    out_specs = P(("row", "sub"), None, None, None)
    return jax.shard_map(body, mesh=mesh, in_specs=in_specs, out_specs=out_specs, check_vma=False)
```

time: 532 us -> 180 us (0.34)
  waiting for transfers between devices: 290 us -> 67.5 us
  matrix products: 97.3 us -> 0.63 us
  local copies, waits for them, and re-layouts: 84.4 us -> 6 us
  Pallas kernels: 0 us -> 63.6 us
  other arithmetic: 36.8 us -> 5.45 us
  starting transfers between devices: 7.91 us -> 33.2 us
  between operations: 13.5 us -> 0.49 us
    psum x1 -> x0, waiting for transfers between devices: 150 us -> none  [body(): gram = lax.psum(partial_value, ('row', 'sub'))]
    dot_general x19 -> x1, matrix products: 97.3 us -> 0.63 us  [body(): jnp.dot(picked, levels, precision=highest, preferred_element_type=jnp.flo...]
    ppermute x4 -> x29, waiting for transfers between devices: 141 us -> 67.5 us  [the longest x3 16.6 us: body(): far = [lax.ppermute(t, 'row', PASS_ON) for t in near]]
    pallas_call x0 -> x6, Pallas kernels: none -> 63.6 us  [the longest x3 41.3 us: pair_call(): pl.pallas_call(functools.partial(pair_kernel, counts, n_own, group), out_...]
    gather x16 -> x0, local copies, waits for them, and re-layouts: 41.1 us -> none  [one_block(): picked = jnp.take(lookup_table, listed, axis=0)]
    dynamic_update_slice x32 -> x0, local copies, waits for them, and re-layouts: 37.3 us -> none  [body(): return lax.map(one_block, (adj_blocks, flat_index))]
    concatenate x2, other arithmetic: 36.2 us -> 0.65 us  [the longest x1 0.64 us: body(): bounds = jnp.concatenate([starts, limits])]
    ppermute x4 -> x29, starting transfers between devices: 7.91 us -> 33.2 us  [the longest x3 7.13 us: body(): sub_low = [lax.ppermute(t, 'sub', ring(N_SUB, 1)) for t in turned]]
  transfers between devices with their start and end apart: 5 -> 29, of which waited for: 4 -> 17; matrix products, arithmetic and copies ran while one was open for 6% -> 5% of each run, Pallas kernels for 0% -> 27%
where the time goes in v1:
time: 180 us; the launch traced here: 177 us
  waiting for transfers between devices  67.5 us (38%)
  Pallas kernels  63.6 us (35%)
  starting transfers between devices  33.2 us (18%)
  local copies, waits for them, and re-layouts  6 us (3%)
  other arithmetic  5.45 us (3%)
    pallas_call x3, Pallas kernels, pair_call(): pl.pallas_call(functools.partial(pair_kernel, counts, n_own, group), out_...  41.3 us
    ppermute x3, waiting for transfers between devices, body(): far = [lax.ppermute(t, 'row', PASS_ON) for t in near]  16.6 us
    ppermute x3, waiting for transfers between devices, body(): sub_low = [lax.ppermute(t, 'sub', ring(N_SUB, 1)) for t in turned]  14.7 us
    ppermute x3, waiting for transfers between devices, body(): sub_high = [lax.ppermute(t, 'sub', ring(N_SUB, -1)) for t in turned]  13 us
    pallas_call x1, Pallas kernels, adjoint(): pl.pallas_call(adjoint_kernel, out_shape=jax.ShapeDtypeStruct((count, 2 *...  10.9 us
    pallas_call x1, Pallas kernels, front(): pl.pallas_call(functools.partial(front_kernel, spans), out_shape=[jax.Sha...  8.96 us
    ppermute x3, starting transfers between devices, body(): sub_low = [lax.ppermute(t, 'sub', ring(N_SUB, 1)) for t in turned]  7.13 us
    ppermute x3, starting transfers between devices, body(): lax.ppermute(part(total, (z + s) % N_Z, piece), 'row', row_shift(s, 0))  6.57 us
  transfers between devices with their start and end apart: 29, of which 17 were waited for; matrix products, arithmetic and copies ran while one was open for 5% of the time, Pallas kernels for 27%

profile of v1, /device:TPU:24, one launch (start us, length us, event | category | flops | bytes accessed | tf_op | source)
XLA Modules:
  0.0 176.9 jit_solution(10954606829600848755)
XLA Ops:
  0.0 9.0 %front.1 = (f32[7,512,128]{2,1,0:T(8,128)}, f32[3,512,128]{2,1,0:T(8,128)}, bf16[16,512,256]{2,1,0:T(8,128)(2,1)}, f32[512,512]{1,0:T(8,128)}) custom-call(f32[16,128,512]{2,1,0:T(8,128)} %bitcast.10, f32[16,128,512]{2,1,0:T(8,128)} %bitcast.14), custom_call_target="tpu_custom_call" | custom-call | flops 3221225472 | bytes 16777216 | tf_op jit(solution)/shard_map/front/pallas_call | solution.py:152
  10.2 1.8 %collective-permute-done = f32[256,512]{1,0:T(8,128)S(1)} collective-permute-done((f32[256,512]{1,0:T(8,128)S(1)}, f32[256,512]{1,0:T(8,128)S(1)}, u32[]{:S(2)}, u32[]{:S(2)}) %collective-permute-start) | collective-permute-done | bytes 524320 | tf_op jit(solution)/shard_map/ppermute | solution.py:365
  12.0 1.1 dynamic-slice_add_fusion
  13.2 1.6 collective-permute-start.1
  14.8 2.7 %collective-permute-start.2 = (f32[64,512]{1,0:T(8,128)S(1)}, f32[64,512]{1,0:T(8,128)S(1)}, u32[]{:S(2)}, u32[]{:S(2)}) collective-permute-start(f32[64,512]{1,0:T(8,128)S(1)} %get-tuple-element.19), channel_id=1, source_target_pairs={{0,16},{4,20},{8,24},{12,28},{16,0},{20,4},{24,8},{28,12},{32,48},... | collective-permute-start | bytes 393224 | tf_op jit(solution)/shard_map/ppermute | solution.py:371
  17.5 1.4 collective-permute-start.3
  20.1 3.8 %collective-permute-done.2 = f32[64,512]{1,0:T(8,128)S(1)} collective-permute-done((f32[64,512]{1,0:T(8,128)S(1)}, f32[64,512]{1,0:T(8,128)S(1)}, u32[]{:S(2)}, u32[]{:S(2)}) %collective-permute-start.2) | collective-permute-done | bytes 131104 | tf_op jit(solution)/shard_map/ppermute | solution.py:371
  23.9 2.0 %collective-permute-start.4 = (f32[16,512]{1,0:T(8,128)S(1)}, f32[16,512]{1,0:T(8,128)S(1)}, u32[]{:S(2)}, u32[]{:S(2)}) collective-permute-start(f32[16,512]{1,0:T(8,128)S(1)} %get-tuple-element.20), channel_id=1, source_target_pairs={{0,32},{4,36},{8,40},{12,44},{16,48},{20,52},{24,56},{28,60},{32,6... | collective-permute-start | bytes 98312 | tf_op jit(solution)/shard_map/ppermute | solution.py:376
  25.9 3.6 %collective-permute-start.5 = (f32[16,512]{1,0:T(8,128)S(1)}, f32[16,512]{1,0:T(8,128)S(1)}, u32[]{:S(2)}, u32[]{:S(2)}) collective-permute-start(f32[16,512]{1,0:T(8,128)S(1)} %get-tuple-element.22), channel_id=1, source_target_pairs={{0,64},{4,68},{8,72},{12,76},{16,80},{20,84},{24,88},{28,92},{32,9... | collective-permute-start | bytes 98312 | tf_op jit(solution)/shard_map/ppermute | solution.py:376
  30.5 2.6 %turn.1 = f32[6,512,128]{2,1,0:T(8,128)} custom-call(f32[16,128,512]{2,1,0:T(8,128)} %bitcast.11), custom_call_target="tpu_custom_call" | custom-call | flops 1000000000 | bytes 3145728 | tf_op jit(solution)/shard_map/turn/pallas_call | solution.py:71
  33.7 2.6 %collective-permute-start.8 = (f32[16,512]{1,0:T(8,128)S(1)}, f32[16,512]{1,0:T(8,128)S(1)}, u32[]{:S(2)}, u32[]{:S(2)}) collective-permute-start(f32[16,512]{1,0:T(8,128)S(1)} %add_add_fusion.2), channel_id=1, source_target_pairs={{0,2},{1,3},{2,0},{3,1},{4,6},{5,7},{6,4},{7,5},{8,10},{9,11},{10,... | collective-permute-start | bytes 98312 | tf_op jit(solution)/shard_map/ppermute | solution.py:379
  36.3 1.1 collective-permute-done.7
  37.4 1.7 collective-permute-done.8
  39.1 2.3 %collective-permute-done.9 = f32[16,512]{1,0:T(8,128)S(1)} collective-permute-done((f32[16,512]{1,0:T(8,128)S(1)}, f32[16,512]{1,0:T(8,128)S(1)}, u32[]{:S(2)}, u32[]{:S(2)}) %collective-permute-start.9) | collective-permute-done | bytes 32800 | tf_op jit(solution)/shard_map/ppermute | solution.py:379
  42.9 2.9 %collective-permute-start.11 = (f32[16,512]{1,0:T(8,128)S(1)}, f32[16,512]{1,0:T(8,128)S(1)}, u32[]{:S(2)}, u32[]{:S(2)}) collective-permute-start(f32[16,512]{1,0:T(8,128)S(1)} %get-tuple-element.14), channel_id=1, source_target_pairs={{0,64},{4,68},{8,72},{12,76},{16,80},{20,84},{24,88},{28,92},{32,9... | collective-permute-start | bytes 98312 | tf_op jit(solution)/shard_map/ppermute | solution.py:380
  48.3 1.4 collective-permute-done.12
  49.7 1.4 collective-permute-start.13
  51.1 2.4 %collective-permute-start.14 = (f32[64,512]{1,0:T(8,128)S(1)}, f32[64,512]{1,0:T(8,128)S(1)}, u32[]{:S(2)}, u32[]{:S(2)}) collective-permute-start(f32[64,512]{1,0:T(8,128)S(1)} %pad_maximum_fusion), channel_id=1, source_target_pairs={{0,16},{4,20},{8,24},{12,28},{16,0},{20,4},{24,8},{28,12},{32,48},... | collective-permute-start | bytes 393224 | tf_op jit(solution)/shard_map/ppermute | solution.py:381
  53.5 2.5 %collective-permute-done.13 = f32[64,512]{1,0:T(8,128)S(1)} collective-permute-done((f32[64,512]{1,0:T(8,128)S(1)}, f32[64,512]{1,0:T(8,128)S(1)}, u32[]{:S(2)}, u32[]{:S(2)}) %collective-permute-start.13) | collective-permute-done | bytes 131104 | tf_op jit(solution)/shard_map/ppermute | solution.py:381
  57.8 3.1 %collective-permute-done.15 = f32[64,512]{1,0:T(8,128)S(1)} collective-permute-done((f32[64,512]{1,0:T(8,128)S(1)}, f32[64,512]{1,0:T(8,128)S(1)}, u32[]{:S(2)}, u32[]{:S(2)}) %collective-permute-start.15) | collective-permute-done | bytes 131104 | tf_op jit(solution)/shard_map/ppermute | solution.py:381
  64.9 1.9 %collective-permute-done.16.other = f32[256,512]{1,0:T(8,128)S(1)} collective-permute-done((f32[256,512]{1,0:T(8,128)}, f32[256,512]{1,0:T(8,128)S(1)}, u32[]{:S(2)}, u32[]{:S(2)}) %collective-permute-start.16) | collective-permute-done | bytes 524320 | tf_op jit(solution)/shard_map/ppermute | solution.py:382
  66.8 3.2 %collective-permute-start.23 = (f32[7,512,128]{2,1,0:T(8,128)}, f32[7,512,128]{2,1,0:T(8,128)}, u32[]{:S(2)}, u32[]{:S(2)}) collective-permute-start(f32[7,512,128]{2,1,0:T(8,128)} %get-tuple-element.11), channel_id=1, source_target_pairs={{0,1},{1,2},{2,3},{3,0},{4,5},{5,6},{6,7},{7,4},{8,9},{9,10},{10,1... | collective-permute-start | bytes 5505032 | tf_op jit(solution)/shard_map/ppermute | solution.py:359
  70.0 14.7 %collective-permute-done.27.refs_4_ = f32[6,512,128]{2,1,0:T(8,128)} collective-permute-done((f32[6,512,128]{2,1,0:T(8,128)}, f32[6,512,128]{2,1,0:T(8,128)}, u32[]{:S(2)}, u32[]{:S(2)}) %collective-permute-start.27) | collective-permute-done | bytes 1572896 | tf_op jit(solution)/shard_map/ppermute | solution.py:359
  84.8 1.4 collective-permute-start.20
  86.6 13.0 %collective-permute-done.28.refs_5_ = f32[6,512,128]{2,1,0:T(8,128)} collective-permute-done((f32[6,512,128]{2,1,0:T(8,128)}, f32[6,512,128]{2,1,0:T(8,128)}, u32[]{:S(2)}, u32[]{:S(2)}) %collective-permute-start.28) | collective-permute-done | bytes 1572896 | tf_op jit(solution)/shard_map/ppermute | solution.py:360
  102.0 1.2 subtract_divide_fusion.factor
  103.2 16.6 %collective-permute-done.22.refs_1_ = f32[3,512,128]{2,1,0:T(8,128)S(1)} collective-permute-done((f32[3,512,128]{2,1,0:T(8,128)S(1)}, f32[3,512,128]{2,1,0:T(8,128)S(1)}, u32[]{:S(2)}, u32[]{:S(2)}) %collective-permute-start.22) | collective-permute-done | bytes 786464 | tf_op jit(solution)/shard_map/ppermute | solution.py:362
  120.7 3.2 %collective-permute-start.17 = (f32[3,512,128]{2,1,0:T(8,128)}, f32[3,512,128]{2,1,0:T(8,128)}, u32[]{:S(2)}, u32[]{:S(2)}) collective-permute-start(f32[3,512,128]{2,1,0:T(8,128)} %get-tuple-element.10), channel_id=1, source_target_pairs={{0,1},{1,2},{2,3},{3,0},{4,5},{5,6},{6,7},{7,4},{8,9},{9,10},{10,1... | collective-permute-start | bytes 2359304 | tf_op jit(solution)/shard_map/ppermute | solution.py:359
  124.5 10.9 %adjoint.1.adjoint_blocks = bf16[16,256,512]{2,1,0:T(8,128)(2,1)} custom-call(s32[3]{0:T(128)} %pad_add_fusion.1.place, f32[16,128,512]{2,1,0:T(8,128)} %bitcast.12, f32[256,512]{1,0:T(8,128)} %constant_dynamic-update-slice_fusion.mine, f32[256,512]{1,0:T(8,128)} %copy-done.6, f32[512,512]{1,0:T(8,128)} %subtract_divide_fusion.factor), custom_call_target="tpu_custom_call" | custom-call | flops 3221225472 | bytes 8388608 | tf_op jit(solution)/shard_map/adjoint/pallas_call | solution.py:214
  135.4 22.5 %shard_map.64.refs_4_ = f32[192,128,128]{2,1,0:T(8,128)} custom-call(s32[16]{0:T(128)} %pad_add_fusion.bounds, s32[192]{0:T(256)} %select_reduce_fusion.keys, bf16[16,256,512]{2,1,0:T(8,128)(2,1)} %adjoint.1.adjoint_blocks, f32[6,512,128]{2,1,0:T(8,128)} %collective-permute-done.25.refs_0_, f32[7,512,128]{2,1,0:T(8,128)} %copy-done.1, ...), custom_call_target="tpu_custom_call" | custom-call | flops 3355443200 | bytes 8388608 | tf_op jit(solution)/shard_map/pallas_call | solution.py:320
  157.9 12.3 %shard_map.65.refs_2_ = f32[192,128,128]{2,1,0:T(8,128)} custom-call(s32[16]{0:T(128)} %pad_add_fusion.bounds, s32[192]{0:T(256)} %select_reduce_fusion.keys, bf16[16,256,512]{2,1,0:T(8,128)(2,1)} %adjoint.1.adjoint_blocks, f32[7,512,128]{2,1,0:T(8,128)} %collective-permute-done.20.refs_0_, ...), custom_call_target="tpu_custom_call", output_to_operand_aliasing={{}: (7, {})} | custom-call | flops 1610612736 | bytes 8388608 | tf_op jit(solution)/shard_map/pallas_call | solution.py:320
  170.3 6.5 %shard_map.66 = f32[192,128,128]{2,1,0:T(8,128)} custom-call(s32[16]{0:T(128)} %pad_add_fusion.bounds, s32[192]{0:T(256)} %select_reduce_fusion.keys, bf16[16,256,512]{2,1,0:T(8,128)(2,1)} %adjoint.1.adjoint_blocks, f32[3,512,128]{2,1,0:T(8,128)} %collective-permute-done.17.refs_0_, ...), custom_call_target="tpu_custom_call", output_to_operand_aliasing={{}: (5, {})} | custom-call | flops 402653184 | bytes 8388608 | tf_op jit(solution)/shard_map/pallas_call | solution.py:320
  (73 shorter events, 18.1 us)
Async XLA Ops:
  0.0 101.3 %copy-start = (f32[512]{0:T(512)S(1)}, f32[512]{0:T(512)}, u32[]{:S(2)}) copy-start(f32[512]{0:T(512)} %param.8) | copy-start | bytes 6148
  10.1 2.0 %collective-permute-start = (f32[256,512]{1,0:T(8,128)S(1)}, f32[256,512]{1,0:T(8,128)S(1)}, u32[]{:S(2)}, u32[]{:S(2)}) collective-permute-start(f32[256,512]{1,0:T(8,128)S(1)} %constant_dynamic-slice_fusion.6), channel_id=1, source_target_pairs={{0,4},{4,0},{8,12},{12,8},{16,20},{20,16},{24,28},{28,24},{32,36},... | collective-permute-start | bytes 1572872 | tf_op jit(solution)/shard_map/ppermute | solution.py:365
  13.2 6.8 %collective-permute-start.1 = (f32[64,512]{1,0:T(8,128)S(1)}, f32[64,512]{1,0:T(8,128)S(1)}, u32[]{:S(2)}, u32[]{:S(2)}) collective-permute-start(f32[64,512]{1,0:T(8,128)S(1)} %get-tuple-element.17), channel_id=1, source_target_pairs={{0,8},{4,12},{8,16},{12,20},{16,24},{20,28},{24,0},{28,4},{32,40},... | collective-permute-start | bytes 393224 | tf_op jit(solution)/shard_map/ppermute | solution.py:371
  14.8 9.1 %collective-permute-start.2 = (f32[64,512]{1,0:T(8,128)S(1)}, f32[64,512]{1,0:T(8,128)S(1)}, u32[]{:S(2)}, u32[]{:S(2)}) collective-permute-start(f32[64,512]{1,0:T(8,128)S(1)} %get-tuple-element.19), channel_id=1, source_target_pairs={{0,16},{4,20},{8,24},{12,28},{16,0},{20,4},{24,8},{28,12},{32,48},... | collective-permute-start | bytes 393224 | tf_op jit(solution)/shard_map/ppermute | solution.py:371
  17.5 6.3 %collective-permute-start.3 = (f32[64,512]{1,0:T(8,128)S(1)}, f32[64,512]{1,0:T(8,128)S(1)}, u32[]{:S(2)}, u32[]{:S(2)}) collective-permute-start(f32[64,512]{1,0:T(8,128)S(1)} %get-tuple-element.18), channel_id=1, source_target_pairs={{0,24},{4,28},{8,0},{12,4},{16,8},{20,12},{24,16},{28,20},{32,56},... | collective-permute-start | bytes 393224 | tf_op jit(solution)/shard_map/ppermute | solution.py:371
  23.9 9.3 %collective-permute-start.4 = (f32[16,512]{1,0:T(8,128)S(1)}, f32[16,512]{1,0:T(8,128)S(1)}, u32[]{:S(2)}, u32[]{:S(2)}) collective-permute-start(f32[16,512]{1,0:T(8,128)S(1)} %get-tuple-element.20), channel_id=1, source_target_pairs={{0,32},{4,36},{8,40},{12,44},{16,48},{20,52},{24,56},{28,60},{32,6... | collective-permute-start | bytes 98312 | tf_op jit(solution)/shard_map/ppermute | solution.py:376
  25.9 7.3 %collective-permute-start.5 = (f32[16,512]{1,0:T(8,128)S(1)}, f32[16,512]{1,0:T(8,128)S(1)}, u32[]{:S(2)}, u32[]{:S(2)}) collective-permute-start(f32[16,512]{1,0:T(8,128)S(1)} %get-tuple-element.22), channel_id=1, source_target_pairs={{0,64},{4,68},{8,72},{12,76},{16,80},{20,84},{24,88},{28,92},{32,9... | collective-permute-start | bytes 98312 | tf_op jit(solution)/shard_map/ppermute | solution.py:376
  29.5 56.9 %copy-start.5 = (s32[8]{0:T(128)S(1)}, s32[8]{0:T(128)}, u32[]{:S(2)}) copy-start(s32[8]{0:T(128)} %constant.186.clone) | copy-start | bytes 100
  29.5 71.9 %copy-start.7 = (s32[512]{0:T(512)S(1)}, s32[512]{0:T(512)}, u32[]{:S(2)}) copy-start(s32[512]{0:T(512)} %param.9) | copy-start | bytes 6148
  29.5 3.9 %collective-permute-start.6 = (f32[16,512]{1,0:T(8,128)S(1)}, f32[16,512]{1,0:T(8,128)S(1)}, u32[]{:S(2)}, u32[]{:S(2)}) collective-permute-start(f32[16,512]{1,0:T(8,128)S(1)} %get-tuple-element.21), channel_id=1, source_target_pairs={{0,96},{4,100},{8,104},{12,108},{16,112},{20,116},{24,120},{28,124... | collective-permute-start | bytes 98312 | tf_op jit(solution)/shard_map/ppermute | solution.py:376
  33.1 31.6 %collective-permute-start.25 = (f32[6,512,128]{2,1,0:T(8,128)}, f32[6,512,128]{2,1,0:T(8,128)}, u32[]{:S(2)}, u32[]{:S(2)}) collective-permute-start(f32[6,512,128]{2,1,0:T(8,128)} %turn.1), channel_id=1, source_target_pairs={{0,4},{4,0},{8,12},{12,8},{16,20},{20,16},{24,28},{28,24},{32,36},... | collective-permute-start | bytes 4718600 | tf_op jit(solution)/shard_map/ppermute | solution.py:361
  33.4 4.0 %collective-permute-start.7 = (f32[16,512]{1,0:T(8,128)S(1)}, f32[16,512]{1,0:T(8,128)S(1)}, u32[]{:S(2)}, u32[]{:S(2)}) collective-permute-start(f32[16,512]{1,0:T(8,128)S(1)} %add_add_fusion.2), channel_id=1, source_target_pairs={{0,1},{1,2},{2,3},{3,0},{4,5},{5,6},{6,7},{7,4},{8,9},{9,10},{10,1... | collective-permute-start | bytes 98312 | tf_op jit(solution)/shard_map/ppermute | solution.py:379
  33.7 5.4 %collective-permute-start.8 = (f32[16,512]{1,0:T(8,128)S(1)}, f32[16,512]{1,0:T(8,128)S(1)}, u32[]{:S(2)}, u32[]{:S(2)}) collective-permute-start(f32[16,512]{1,0:T(8,128)S(1)} %add_add_fusion.2), channel_id=1, source_target_pairs={{0,2},{1,3},{2,0},{3,1},{4,6},{5,7},{6,4},{7,5},{8,10},{9,11},{10,... | collective-permute-start | bytes 98312 | tf_op jit(solution)/shard_map/ppermute | solution.py:379
  36.3 5.1 %collective-permute-start.9 = (f32[16,512]{1,0:T(8,128)S(1)}, f32[16,512]{1,0:T(8,128)S(1)}, u32[]{:S(2)}, u32[]{:S(2)}) collective-permute-start(f32[16,512]{1,0:T(8,128)S(1)} %add_add_fusion.2), channel_id=1, source_target_pairs={{0,3},{1,0},{2,1},{3,2},{4,7},{5,4},{6,5},{7,6},{8,11},{9,8},{10,9... | collective-permute-start | bytes 98312 | tf_op jit(solution)/shard_map/ppermute | solution.py:379
  36.3 48.4 %collective-permute-start.19 = (f32[7,512,128]{2,1,0:T(8,128)}, f32[7,512,128]{2,1,0:T(8,128)S(1)}, u32[]{:S(2)}, u32[]{:S(2)}) collective-permute-start(f32[7,512,128]{2,1,0:T(8,128)} %get-tuple-element.11), channel_id=1, source_target_pairs={{0,4},{4,0},{8,12},{12,8},{16,20},{20,16},{24,28},{28,24},{32,36},... | collective-permute-start | bytes 5505032 | tf_op jit(solution)/shard_map/ppermute | solution.py:361
  42.1 5.1 %collective-permute-start.10 = (f32[16,512]{1,0:T(8,128)S(1)}, f32[16,512]{1,0:T(8,128)S(1)}, u32[]{:S(2)}, u32[]{:S(2)}) collective-permute-start(f32[16,512]{1,0:T(8,128)S(1)} %get-tuple-element.14), channel_id=1, source_target_pairs={{0,32},{4,36},{8,40},{12,44},{16,48},{20,52},{24,56},{28,60},{32,6... | collective-permute-start | bytes 98312 | tf_op jit(solution)/shard_map/ppermute | solution.py:380
  42.9 5.4 %collective-permute-start.11 = (f32[16,512]{1,0:T(8,128)S(1)}, f32[16,512]{1,0:T(8,128)S(1)}, u32[]{:S(2)}, u32[]{:S(2)}) collective-permute-start(f32[16,512]{1,0:T(8,128)S(1)} %get-tuple-element.14), channel_id=1, source_target_pairs={{0,64},{4,68},{8,72},{12,76},{16,80},{20,84},{24,88},{28,92},{32,9... | collective-permute-start | bytes 98312 | tf_op jit(solution)/shard_map/ppermute | solution.py:380
  45.7 3.9 %collective-permute-start.12 = (f32[16,512]{1,0:T(8,128)S(1)}, f32[16,512]{1,0:T(8,128)S(1)}, u32[]{:S(2)}, u32[]{:S(2)}) collective-permute-start(f32[16,512]{1,0:T(8,128)S(1)} %get-tuple-element.14), channel_id=1, source_target_pairs={{0,96},{4,100},{8,104},{12,108},{16,112},{20,116},{24,120},{28,124... | collective-permute-start | bytes 98312 | tf_op jit(solution)/shard_map/ppermute | solution.py:380
  47.2 37.6 %collective-permute-start.27 = (f32[6,512,128]{2,1,0:T(8,128)}, f32[6,512,128]{2,1,0:T(8,128)}, u32[]{:S(2)}, u32[]{:S(2)}) collective-permute-start(f32[6,512,128]{2,1,0:T(8,128)} %turn.1), channel_id=1, source_target_pairs={{0,1},{1,2},{2,3},{3,0},{4,5},{5,6},{6,7},{7,4},{8,9},{9,10},{10,1... | collective-permute-start | bytes 4718600 | tf_op jit(solution)/shard_map/ppermute | solution.py:359
  49.7 6.2 %collective-permute-start.13 = (f32[64,512]{1,0:T(8,128)S(1)}, f32[64,512]{1,0:T(8,128)S(1)}, u32[]{:S(2)}, u32[]{:S(2)}) collective-permute-start(f32[64,512]{1,0:T(8,128)S(1)} %pad_maximum_fusion), channel_id=1, source_target_pairs={{0,8},{4,12},{8,16},{12,20},{16,24},{20,28},{24,0},{28,4},{32,40},... | collective-permute-start | bytes 393224 | tf_op jit(solution)/shard_map/ppermute | solution.py:381
  51.1 6.7 %collective-permute-start.14 = (f32[64,512]{1,0:T(8,128)S(1)}, f32[64,512]{1,0:T(8,128)S(1)}, u32[]{:S(2)}, u32[]{:S(2)}) collective-permute-start(f32[64,512]{1,0:T(8,128)S(1)} %pad_maximum_fusion), channel_id=1, source_target_pairs={{0,16},{4,20},{8,24},{12,28},{16,0},{20,4},{24,8},{28,12},{32,48},... | collective-permute-start | bytes 393224 | tf_op jit(solution)/shard_map/ppermute | solution.py:381
  55.9 5.0 %collective-permute-start.15 = (f32[64,512]{1,0:T(8,128)S(1)}, f32[64,512]{1,0:T(8,128)S(1)}, u32[]{:S(2)}, u32[]{:S(2)}) collective-permute-start(f32[64,512]{1,0:T(8,128)S(1)} %pad_maximum_fusion), channel_id=1, source_target_pairs={{0,24},{4,28},{8,0},{12,4},{16,8},{20,12},{24,16},{28,20},{32,56},... | collective-permute-start | bytes 393224 | tf_op jit(solution)/shard_map/ppermute | solution.py:381
  57.8 6.9 %collective-permute-start.21 = (f32[3,512,128]{2,1,0:T(8,128)}, f32[3,512,128]{2,1,0:T(8,128)S(1)}, u32[]{:S(2)}, u32[]{:S(2)}) collective-permute-start(f32[3,512,128]{2,1,0:T(8,128)} %get-tuple-element.10), channel_id=1, source_target_pairs={{0,4},{4,0},{8,12},{12,8},{16,20},{20,16},{24,28},{28,24},{32,36},... | collective-permute-start | bytes 2359304 | tf_op jit(solution)/shard_map/ppermute | solution.py:361
  60.9 38.8 %collective-permute-start.28 = (f32[6,512,128]{2,1,0:T(8,128)}, f32[6,512,128]{2,1,0:T(8,128)}, u32[]{:S(2)}, u32[]{:S(2)}) collective-permute-start(f32[6,512,128]{2,1,0:T(8,128)} %turn.1), channel_id=1, source_target_pairs={{0,3},{1,0},{2,1},{3,2},{4,7},{5,4},{6,5},{7,6},{8,11},{9,8},{10,9... | collective-permute-start | bytes 4718600 | tf_op jit(solution)/shard_map/ppermute | solution.py:360
  64.7 2.1 %collective-permute-start.16 = (f32[256,512]{1,0:T(8,128)}, f32[256,512]{1,0:T(8,128)S(1)}, u32[]{:S(2)}, u32[]{:S(2)}) collective-permute-start(f32[256,512]{1,0:T(8,128)} %constant_dynamic-update-slice_fusion.mine), channel_id=1, source_target_pairs={{0,4},{4,0},{8,12},{12,8},{16,20},{20,16},{24,28},{28,24},{32,36},... | collective-permute-start | bytes 1572872 | tf_op jit(solution)/shard_map/ppermute | solution.py:382
  64.7 59.2 %collective-permute-start.26 = (f32[6,512,128]{2,1,0:T(8,128)}, f32[6,512,128]{2,1,0:T(8,128)}, u32[]{:S(2)}, u32[]{:S(2)}) collective-permute-start(f32[6,512,128]{2,1,0:T(8,128)} %collective-permute-done.25.refs_0_), channel_id=1, source_target_pairs={{0,8},{4,124},{8,16},{12,4},{16,24},{20,12},{24,32},{28,20},{32,40... | collective-permute-start | bytes 4718600 | tf_op jit(solution)/shard_map/ppermute | solution.py:362
  66.8 91.1 %collective-permute-start.23 = (f32[7,512,128]{2,1,0:T(8,128)}, f32[7,512,128]{2,1,0:T(8,128)}, u32[]{:S(2)}, u32[]{:S(2)}) collective-permute-start(f32[7,512,128]{2,1,0:T(8,128)} %get-tuple-element.11), channel_id=1, source_target_pairs={{0,1},{1,2},{2,3},{3,0},{4,5},{5,6},{6,7},{7,4},{8,9},{9,10},{10,1... | collective-permute-start | bytes 5505032 | tf_op jit(solution)/shard_map/ppermute | solution.py:359
  84.8 73.2 %collective-permute-start.24 = (f32[7,512,128]{2,1,0:T(8,128)}, f32[7,512,128]{2,1,0:T(8,128)}, u32[]{:S(2)}, u32[]{:S(2)}) collective-permute-start(f32[7,512,128]{2,1,0:T(8,128)} %get-tuple-element.11), channel_id=1, source_target_pairs={{0,3},{1,0},{2,1},{3,2},{4,7},{5,4},{6,5},{7,6},{8,11},{9,8},{10,9... | collective-permute-start | bytes 5505032 | tf_op jit(solution)/shard_map/ppermute | solution.py:360
  84.8 73.1 %collective-permute-start.20 = (f32[7,512,128]{2,1,0:T(8,128)S(1)}, f32[7,512,128]{2,1,0:T(8,128)}, u32[]{:S(2)}, u32[]{:S(2)}) collective-permute-start(f32[7,512,128]{2,1,0:T(8,128)S(1)} %collective-permute-done.19.refs_1_), channel_id=1, source_target_pairs={{0,8},{4,124},{8,16},{12,4},{16,24},{20,12},{24,32},{28,20},{32,40... | collective-permute-start | bytes 5505032 | tf_op jit(solution)/shard_map/ppermute | solution.py:362
  99.7 20.1 %collective-permute-start.22 = (f32[3,512,128]{2,1,0:T(8,128)S(1)}, f32[3,512,128]{2,1,0:T(8,128)S(1)}, u32[]{:S(2)}, u32[]{:S(2)}) collective-permute-start(f32[3,512,128]{2,1,0:T(8,128)S(1)} %collective-permute-done.21.refs_2_), channel_id=1, source_target_pairs={{0,8},{4,124},{8,16},{12,4},{16,24},{20,12},{24,32},{28,20},{32,40... | collective-permute-start | bytes 2359304 | tf_op jit(solution)/shard_map/ppermute | solution.py:362
  120.7 49.6 %collective-permute-start.17 = (f32[3,512,128]{2,1,0:T(8,128)}, f32[3,512,128]{2,1,0:T(8,128)}, u32[]{:S(2)}, u32[]{:S(2)}) collective-permute-start(f32[3,512,128]{2,1,0:T(8,128)} %get-tuple-element.10), channel_id=1, source_target_pairs={{0,1},{1,2},{2,3},{3,0},{4,5},{5,6},{6,7},{7,4},{8,9},{9,10},{10,1... | collective-permute-start | bytes 2359304 | tf_op jit(solution)/shard_map/ppermute | solution.py:359
  123.9 46.3 %collective-permute-start.18 = (f32[3,512,128]{2,1,0:T(8,128)}, f32[3,512,128]{2,1,0:T(8,128)}, u32[]{:S(2)}, u32[]{:S(2)}) collective-permute-start(f32[3,512,128]{2,1,0:T(8,128)} %get-tuple-element.10), channel_id=1, source_target_pairs={{0,3},{1,0},{2,1},{3,2},{4,7},{5,4},{6,5},{7,6},{8,11},{9,8},{10,9... | collective-permute-start | bytes 2359304 | tf_op jit(solution)/shard_map/ppermute | solution.py:360
  (5 other events, 161.2 us)

commit v2 on v1

v2 whole, which is shorter than its diff:
```python
import functools

import jax
import jax.numpy as jnp
from jax import lax
from jax.experimental import pallas as pl
from jax.experimental.pallas import tpu as pltpu
from jax.sharding import PartitionSpec as P


BS = 128
broadening_sq = 0.0025

N_CORE, N_X, N_Z = 2, 4, 4
N_ROW, N_SUB = N_CORE * N_X * N_Z, 4

SUB_PIECES = (6, 7, 3)
ROW_PIECES = (4, 6, 4, 2)
STAGES, UNROLL, STEP = 16, 8, 4
WHOLE_VMEM = 62 * 2**20
SELF, NEAR, FAR, SUB_LOW, SUB_HIGH = range(5)


def row_shift(dz, dx):
    pairs = []
    for r in range(N_ROW):
        core, x, z = r % N_CORE, (r // N_CORE) % N_X, r // (N_CORE * N_X)
        target = (((z + dz) % N_Z) * N_X + (x + dx) % N_X) * N_CORE + core
        pairs.append((r, target))
    return pairs


CORE_SWAP = [(r, r ^ 1) for r in range(N_ROW)]


PASS_ON = [(r, (r + (-2 if r % 2 else 2)) % N_ROW) for r in range(N_ROW)]


def ring(count, step):
    return [(i, (i + step) % count) for i in range(count)]


def part(array, index, size):
    return lax.dynamic_slice_in_dim(array, index * size, size, axis=0)


def gather_back(mine, count, send):
    return jnp.concatenate([mine] + [send(step) for step in range(1, count)])


def split(value):
    high = value.astype(jnp.bfloat16)
    return high, (value - high.astype(jnp.float32)).astype(jnp.bfloat16)


def turn_kernel(spans, blocks, *refs):
    n_out = len(spans)
    outs = refs[:n_out]
    q, turned, q_sems, t_sems = refs[n_out:]
    low = min(first for first, _ in spans)
    count = q.shape[0]

    def fetch(b):
        return pltpu.make_async_copy(blocks.at[low + b], q.at[b], q_sems.at[b])

    def store(n, b):
        at = low + b - spans[n][0]
        return pltpu.make_async_copy(turned.at[b], outs[n].at[at], t_sems.at[n, b])

    for b in range(count):
        fetch(b).start()

    def step(b, _):
        fetch(b).wait()
        turned[b] = q[b].T
        for n, (first, last) in enumerate(spans):

            @pl.when((low + b >= first) & (low + b < last))
            def _(n=n):
                store(n, b).start()

        return 0

    lax.fori_loop(0, count, step, 0)
    for n, (first, last) in enumerate(spans):
        for b in range(first, last):
            store(n, b - low).wait()


def turn(blocks, spans):
    _, rows, window = blocks.shape
    count = max(last for _, last in spans) - min(first for first, _ in spans)
    hbm = pl.BlockSpec(memory_space=pltpu.HBM)
    return pl.pallas_call(
        functools.partial(turn_kernel, spans),
        out_shape=[
            jax.ShapeDtypeStruct((last - first, window, rows), jnp.float32)
            for first, last in spans
        ],
        in_specs=[hbm],
        out_specs=[hbm] * len(spans),
        scratch_shapes=[
            pltpu.VMEM((count, rows, window), jnp.float32),
            pltpu.VMEM((count, window, rows), jnp.float32),
            pltpu.SemaphoreType.DMA((count,)),
            pltpu.SemaphoreType.DMA((len(spans), count)),
        ],
        compiler_params=pltpu.CompilerParams(vmem_limit_bytes=WHOLE_VMEM),
        cost_estimate=pl.CostEstimate(
            flops=10**9, bytes_accessed=2 * count * rows * window * 4, transcendentals=0
        ),
    )(blocks)


def gram_kernel(place, blocks, other, kept, sent, q, v, gram, q_sems, v_sems):
    count = blocks.shape[0]

    def fetch(b):
        return (
            pltpu.make_async_copy(blocks.at[b], q.at[b], q_sems.at[b]),
            pltpu.make_async_copy(other.at[b], v.at[b], v_sems.at[b]),
        )

    for b in range(count):
        for copy in fetch(b):
            copy.start()
    gram[...] = jnp.zeros_like(gram)

    def step(n, _):
        for u in range(STEP):
            for copy in fetch(n * STEP + u):
                copy.wait()
        left, right = [], []
        for u in range(STEP):
            b = n * STEP + u
            high, low = split(q[b].T)
            vh, vl = split(v[b])
            left += [high, high, low]
            right += [vh, vl, vh]
        gram[...] += jnp.dot(
            jnp.concatenate(left, axis=1),
            jnp.concatenate(right, axis=0),
            preferred_element_type=jnp.float32,
        )
        return 0

    lax.fori_loop(0, count // STEP, step, 0)
    half = kept.shape[0]
    core = place[0]
    kept[...] = gram[pl.ds(pl.multiple_of(core * half, half), half), :]
    sent[...] = gram[pl.ds(pl.multiple_of((1 - core) * half, half), half), :]


def local_gram(place, blocks, other):
    count, rows, window = blocks.shape
    hbm = pl.BlockSpec(memory_space=pltpu.HBM)
    return pl.pallas_call(
        gram_kernel,
        out_shape=[jax.ShapeDtypeStruct((window // N_CORE, window), jnp.float32)] * 2,
        in_specs=[pl.BlockSpec(memory_space=pltpu.SMEM), hbm, hbm],
        out_specs=[pl.BlockSpec(memory_space=pltpu.VMEM)] * 2,
        scratch_shapes=[pltpu.VMEM((count, rows, window), jnp.float32)] * 2
        + [pltpu.VMEM((window, window), jnp.float32)]
        + [pltpu.SemaphoreType.DMA((count,))] * 2,
        compiler_params=pltpu.CompilerParams(vmem_limit_bytes=WHOLE_VMEM),
        cost_estimate=pl.CostEstimate(
            flops=6 * count * rows * window * window, bytes_accessed=2**23, transcendentals=0
        ),
        name="gram",
    )(place, blocks, other)


def weigh(place, mine, other, factor, sh, sl):
    half = mine.shape[0]
    core, x, z = place[0], place[1], place[2]
    size = half // (N_X * N_Z)
    for index, ref in enumerate((mine, other)):
        start = jnp.where(core == index, 0, half)
        for i in range(N_X):
            for j in range(N_Z):
                at = start + (lax.rem(x + N_X - i, N_X) * N_Z + lax.rem(z + N_Z - j, N_Z)) * size
                rows = pl.ds(pl.multiple_of(at, size), size)
                part_of = ref[(i * N_Z + j) * size : (i * N_Z + j + 1) * size, :]
                sh[rows, :], sl[rows, :] = split(factor[rows, :] * part_of)


def make_adjoints(fetch, q, sh, sl, adjoints, keep):
    def some(n, _):
        for u in range(STEP):
            fetch(n * STEP + u).wait()
        highs, lows = zip(*[split(q[n * STEP + u]) for u in range(STEP)])
        tall = STEP * BS
        first = jnp.dot(
            jnp.concatenate(highs + lows, axis=0), sh[...], preferred_element_type=jnp.float32
        )
        second = jnp.dot(
            jnp.concatenate(highs, axis=0), sl[...], preferred_element_type=jnp.float32
        )
        high, low = split(first[:tall] + (first[tall:] + second))
        for u in range(STEP):
            i = n * STEP + u
            adjoints[i, :BS, :] = high[u * BS : (u + 1) * BS]
            adjoints[i, BS:, :] = low[u * BS : (u + 1) * BS]
        for u in range(STEP):
            keep(n * STEP + u).start()
        return 0

    lax.fori_loop(0, q.shape[0] // STEP, some, 0)


def pair_kernel(counts, group, bounds, keys, *refs):
    n_src, n_blk = len(counts), sum(counts)
    if group == 0:
        place, blocks, mine, other, factor = refs[:5]
        sources = refs[5 : 5 + n_src]
        out, kept_adjoints, adjoints, fetched, stage, sems, fetch_sems = refs[5 + n_src : 12 + n_src]
        q, sh, sl, q_sems, keep_sems = refs[12 + n_src :]
        n_rows = blocks.shape[0]

        def fetch(i):
            return pltpu.make_async_copy(blocks.at[i], q.at[i], q_sems.at[i])

        def keep(i):
            return pltpu.make_async_copy(adjoints.at[i], kept_adjoints.at[i], keep_sems.at[i])

        for i in range(n_rows):
            fetch(i).start()
    else:
        given_adjoints = refs[0]
        sources = refs[1 : 1 + n_src]
        out, adjoints, fetched, stage, sems, fetch_sems, adjoint_sem = refs[2 + n_src :]
        adjoint_copy = pltpu.make_async_copy(given_adjoints, adjoints, adjoint_sem)
    pieces = [(source, b) for source, count in zip(sources, counts) for b in range(count)]
    for n, (source, b) in enumerate(pieces):
        pltpu.make_async_copy(source.at[b], fetched.at[n], fetch_sems.at[n]).start()
    if group == 0:
        weigh(place, mine, other, factor, sh, sl)
        make_adjoints(fetch, q, sh, sl, adjoints, keep)
    else:
        adjoint_copy.start()

    def arrive(n, _):
        pltpu.make_async_copy(sources[0].at[0], fetched.at[n], fetch_sems.at[n]).wait()
        return 0

    lax.fori_loop(0, n_blk, arrive, 0)
    if group:
        adjoint_copy.wait()
    first, last = bounds[group], bounds[group + 1]
    origin = bounds[group + 8]
    total = last - first

    def copy_out(slot, target):
        return pltpu.make_async_copy(stage.at[slot], out.at[target], sems.at[slot])

    def some(step, _):
        at = step * UNROLL
        products = []
        names = [keys[first + at + u] for u in range(UNROLL)]
        for one, two in zip(names[::2], names[1::2]):
            i = (jnp.maximum(one, 0) >> 4) & 15
            b1 = jnp.maximum((one >> 8) - origin, 0)
            b2 = jnp.maximum((two >> 8) - origin, 0)
            rows = adjoints[i]
            h1, l1 = split(fetched[b1])
            h2, l2 = split(fetched[b2])
            by_high = jnp.dot(
                rows,
                jnp.concatenate([h1, h2], axis=1),
                preferred_element_type=jnp.float32,
            )
            by_low = jnp.dot(
                rows[:BS],
                jnp.concatenate([l1, l2], axis=1),
                preferred_element_type=jnp.float32,
            )
            product = by_high[:BS] + (by_high[BS:] + by_low)
            products += [product[:, :BS], product[:, BS:]]
        for u in range(UNROLL):
            slot = lax.rem(at + u, STAGES)
            before = keys[jnp.maximum(first + at + u - STAGES, 0)]

            @pl.when((at + u >= STAGES) & (before >= 0))
            def _():
                copy_out(slot, 0).wait()

            stage[slot] = products[u]

            @pl.when(names[u] >= 0)
            def _():
                copy_out(slot, ((names[u] >> 4) & 15) * 12 + (names[u] & 15)).start()

        return 0

    steps = lax.div(total, UNROLL)
    lax.fori_loop(0, steps, some, 0)
    for s in range(STAGES):
        at = total - STAGES + s

        @pl.when((at >= 0) & (keys[jnp.maximum(first + at, 0)] >= 0))
        def _():
            copy_out(lax.rem(at, STAGES), 0).wait()

    if group == 0:
        for i in range(n_rows):
            keep(i).wait()


def pair_call(group, bounds, keys, sources, out, shape, adjoints, inputs):
    counts = tuple(s.shape[0] for s in sources)
    n_blk = sum(counts)
    window = sources[0].shape[1]
    rows = inputs[1].shape[0]
    smem = pl.BlockSpec(memory_space=pltpu.SMEM)
    vmem = pl.BlockSpec(memory_space=pltpu.VMEM)
    hbm = pl.BlockSpec(memory_space=pltpu.HBM)
    out_shape = [jax.ShapeDtypeStruct(shape, jnp.float32)]
    scratch = [
        pltpu.VMEM((rows, 2 * BS, window), jnp.bfloat16),
        pltpu.VMEM((n_blk, window, BS), jnp.float32),
        pltpu.VMEM((STAGES, BS, BS), jnp.float32),
        pltpu.SemaphoreType.DMA((STAGES,)),
        pltpu.SemaphoreType.DMA((n_blk,)),
    ]
    flops = n_blk * 16 * BS * BS * window
    if group == 0:
        operands = [bounds, keys, *inputs, *sources]
        specs = [smem] * 3 + [hbm] + [vmem] * 3 + [hbm] * len(sources)
        out_shape.append(jax.ShapeDtypeStruct((rows, 2 * BS, window), jnp.bfloat16))
        scratch += [
            pltpu.VMEM((rows, BS, window), jnp.float32),
            pltpu.VMEM((window, window), jnp.bfloat16),
            pltpu.VMEM((window, window), jnp.bfloat16),
            pltpu.SemaphoreType.DMA((rows,)),
            pltpu.SemaphoreType.DMA((rows,)),
        ]
        aliases = {}
    else:
        operands = [bounds, keys, adjoints, *sources, out]
        specs = [smem] * 2 + [hbm] * (len(sources) + 2)
        scratch += [pltpu.SemaphoreType.DMA]
        aliases = {len(operands) - 1: 0}
    results = pl.pallas_call(
        functools.partial(pair_kernel, counts, group),
        out_shape=out_shape,
        in_specs=specs,
        out_specs=[hbm] * len(out_shape),
        scratch_shapes=scratch,
        input_output_aliases=aliases,
        compiler_params=pltpu.CompilerParams(
            vmem_limit_bytes=(32, 18, 14)[group] * 2**20
        ),
        cost_estimate=pl.CostEstimate(
            flops=flops, bytes_accessed=8 * 2**20, transcendentals=0
        ),
    )(*operands)
    return results if group == 0 else (results[0], adjoints)


def body(eig_vectors, vec_cotangent, levels, order, neighbours):
    highest = lax.Precision.HIGHEST
    window = eig_vectors.shape[1]
    local_rows = eig_vectors.shape[0]
    blk_count = local_rows // BS
    n_nbr = neighbours.shape[1]
    my_row, my_sub = lax.axis_index("row"), lax.axis_index("sub")
    core, x, z = my_row % N_CORE, (my_row // N_CORE) % N_X, my_row // (N_CORE * N_X)
    blocks = eig_vectors.reshape(blk_count, BS, window)

    def spans_of(sizes):
        return [(sum(sizes[:n]), sum(sizes[: n + 1])) for n in range(len(sizes))]

    place = jnp.stack([core, x, z]).astype(jnp.int32)
    sub_spans, row_spans = spans_of(SUB_PIECES), spans_of(ROW_PIECES)
    start = turn(blocks, [sub_spans[0], row_spans[0]])
    kept_gram, sent_gram = local_gram(
        place, blocks, vec_cotangent.reshape(blk_count, BS, window)
    )
    rest = list(turn(blocks, sub_spans[1:] + row_spans[1:]))
    sub_own = [start[0]] + rest[: len(SUB_PIECES) - 1]
    row_own = [start[1]] + rest[len(SUB_PIECES) - 1 :]
    sub_low = [lax.ppermute(t, "sub", ring(N_SUB, 1)) for t in sub_own]
    sub_high = [lax.ppermute(t, "sub", ring(N_SUB, -1)) for t in sub_own]
    near = [lax.ppermute(t, "row", CORE_SWAP) for t in row_own]
    far = [lax.ppermute(t, "row", PASS_ON) for t in near]

    half = window // N_CORE
    total = kept_gram + lax.ppermute(sent_gram, "row", CORE_SWAP)
    quarter = half // N_X
    mine = part(total, x, quarter)
    for s in range(1, N_X):
        mine += lax.ppermute(part(total, (x + s) % N_X, quarter), "row", row_shift(0, s))
    piece = quarter // N_Z
    total = mine
    mine = part(total, z, piece)
    for s in range(1, N_Z):
        mine += lax.ppermute(part(total, (z + s) % N_Z, piece), "row", row_shift(s, 0))
    total = mine
    for s in range(1, N_SUB):
        total += lax.ppermute(mine, "sub", ring(N_SUB, s))
    total = gather_back(total, N_Z, lambda s: lax.ppermute(total, "row", row_shift(s, 0)))
    total = gather_back(total, N_X, lambda s: lax.ppermute(total, "row", row_shift(0, s)))
    other = lax.ppermute(total, "row", CORE_SWAP)
    columns = lax.broadcasted_iota(jnp.int32, (window, window), 1)
    picked = (order[:, None] == columns).astype(jnp.float32)
    energy = jnp.dot(picked, levels, precision=highest, preferred_element_type=jnp.float32)
    spread = energy[None, :] - energy[:, None]
    factor = spread / (spread * spread + broadening_sq)

    device = neighbours // blk_count
    local = neighbours % blk_count
    row_delta = (device // N_SUB - my_row + N_ROW) % N_ROW
    sub_delta = (device % N_SUB - my_sub + N_SUB) % N_SUB
    slot = jnp.where(sub_delta == 1, SUB_HIGH, jnp.where(sub_delta == N_SUB - 1, SUB_LOW, SELF))
    slot = jnp.where(row_delta == jnp.where(core == 0, 1, N_ROW - 1), NEAR, slot)
    slot = jnp.where(row_delta == jnp.where(core == 0, N_ROW - 1, 1), FAR, slot)
    own = [(SELF, low, array) for (low, _), array in zip(sub_spans, sub_own)]
    near = [(NEAR, low, array) for (low, _), array in zip(row_spans, near)]
    far = [(FAR, low, array) for (low, _), array in zip(row_spans, far)]
    sub = [
        [(SUB_LOW, low, below), (SUB_HIGH, low, above)]
        for (low, _), below, above in zip(sub_spans, sub_low, sub_high)
    ]
    groups = [
        own + near + [far[0]] + sub[0],
        [far[1]] + sub[1],
        far[2:] + sub[2],
    ]
    position = jnp.zeros_like(slot)
    base, origins = 0, []
    for group in groups:
        origins.append(base)
        for which, low, array in group:
            inside = (slot == which) & (local >= low) & (local < low + array.shape[0])
            position = jnp.where(inside, base + local - low, position)
            base += array.shape[0]
    group_of = sum((position >= o).astype(jnp.int32) for o in origins[1:])
    i_index = lax.broadcasted_iota(jnp.int32, position.shape, 0)
    k_index = lax.broadcasted_iota(jnp.int32, position.shape, 1)
    same = group_of[:, :, None] == group_of[:, None, :]
    before = k_index[:, None, :] < k_index[:, :, None]
    within = jnp.sum((same & before).astype(jnp.int32), axis=2)
    n_groups = len(groups)

    each = jnp.arange(n_groups)
    counts = jnp.sum((group_of[:, :, None] == each).astype(jnp.int32), axis=1)
    room = (counts + 1) // 2 * 2
    earlier = (jnp.arange(blk_count)[:, None] > jnp.arange(blk_count)[None, :]).astype(jnp.int32)
    row_start = jnp.sum(earlier[:, :, None] * room[None, :, :], axis=1)
    sizes = (jnp.sum(room, axis=0) + UNROLL - 1) // UNROLL * UNROLL
    starts = jnp.sum(jnp.where(each[:, None] > each[None, :], sizes[None, :], 0), axis=1)
    table = row_start + starts[None, :]
    place_of = within + jnp.sum(
        jnp.where(group_of[:, :, None] == each, table[:, None, :], 0), axis=2
    )
    key = (position * 256 + i_index * 16 + k_index).reshape(-1)
    n_places = (blk_count * (n_nbr + n_groups) // UNROLL + n_groups) * UNROLL
    places = lax.broadcasted_iota(jnp.int32, (n_places, key.shape[0]), 0)
    found = jnp.where(place_of.reshape(1, -1) == places, key[None, :] + 1, 0)
    keys = jnp.sum(found, axis=1) - 1
    ends = jnp.concatenate([starts, jnp.sum(sizes)[None]])
    bounds = jnp.concatenate(
        [ends, jnp.zeros((8 - n_groups - 1,), jnp.int32), jnp.array(origins, jnp.int32)]
    )

    out = adjoints = None
    shape = (blk_count * n_nbr, BS, BS)
    inputs = [place, blocks, total, other, factor]
    for index, group in enumerate(groups):
        arrays = [g[2] for g in group]
        out, adjoints = pair_call(index, bounds, keys, arrays, out, shape, adjoints, inputs)
    return out.reshape(blk_count, n_nbr, BS, BS)


def solution(mesh):
    in_specs = (P(("row", "sub"), None), P(("row", "sub"), None), P(), P(), P(("row", "sub"), None))
    out_specs = P(("row", "sub"), None, None, None)
    return jax.shard_map(body, mesh=mesh, in_specs=in_specs, out_specs=out_specs, check_vma=False)
```

time: 180 us -> 186 us (1.033)
  the two profiles are of different devices: /device:TPU:24 before, /device:TPU:1 now
where the time goes in v2:
time: 186 us; the launch traced here: 185 us
  waiting for transfers between devices  67.4 us (36%)
  starting transfers between devices  50.9 us (27%)
  Pallas kernels  48.7 us (26%)
  local copies, waits for them, and re-layouts  12 us (6%)
  other arithmetic  5.38 us (3%)
    ppermute x3, waiting for transfers between devices, body(): sub_low = [lax.ppermute(t, 'sub', ring(N_SUB, 1)) for t in sub_own]  55.1 us
    pallas_call x3, Pallas kernels, pair_call(): pl.pallas_call(functools.partial(pair_kernel, counts, group), out_shape=o...  34 us
    unnamed x33, local copies, waits for them, and re-layouts  10.9 us
    ppermute x3, starting transfers between devices, body(): sub_high = [lax.ppermute(t, 'sub', ring(N_SUB, -1)) for t in sub_own]  8.93 us
    ppermute x4, starting transfers between devices, body(): far = [lax.ppermute(t, 'row', PASS_ON) for t in near]  8.25 us
    pallas_call x1, Pallas kernels, local_gram(): pl.pallas_call(gram_kernel, out_shape=[jax.ShapeDtypeStruct((window // N_...  7.69 us
    ppermute x4, starting transfers between devices, body(): near = [lax.ppermute(t, 'row', CORE_SWAP) for t in row_own]  7.32 us
    pallas_call x2, Pallas kernels, turn(): pl.pallas_call(functools.partial(turn_kernel, spans), out_shape=[jax.Shap...  7.02 us
  transfers between devices with their start and end apart: 31, of which 11 were waited for; matrix products, arithmetic and copies ran while one was open for 5% of the time, Pallas kernels for 19%

profile of v2, /device:TPU:1, one launch (start us, length us, event | category | flops | bytes accessed | tf_op | source)
XLA Modules:
  0.0 185.5 jit_solution(9746864009784214210)
XLA Ops:
  0.6 7.7 %gram.1 = (f32[256,512]{1,0:T(8,128)}, f32[256,512]{1,0:T(8,128)}) custom-call(s32[3]{0:T(128)} %pad_add_fusion.1.place.refs_0_, f32[16,128,512]{2,1,0:T(8,128)} %bitcast.11, f32[16,128,512]{2,1,0:T(8,128)} %bitcast.16), custom_call_target="tpu_custom_call" | custom-call | flops 3221225472 | bytes 8388608 | tf_op jit(solution)/shard_map/gram/pallas_call | solution.py:157
  8.3 1.5 collective-permute-start
  9.8 1.7 collective-permute-done
  12.7 1.4 collective-permute-start.1
  14.1 2.5 %collective-permute-start.2 = (f32[64,512]{1,0:T(8,128)S(1)}, f32[64,512]{1,0:T(8,128)S(1)}, u32[]{:S(2)}, u32[]{:S(2)}) collective-permute-start(f32[64,512]{1,0:T(8,128)S(1)} %get-tuple-element.37), channel_id=1, source_target_pairs={{0,16},{4,20},{8,24},{12,28},{16,0},{20,4},{24,8},{28,12},{32,48},... | collective-permute-start | bytes 393224 | tf_op jit(solution)/shard_map/ppermute | solution.py:392
  17.7 4.3 %shard_map.65 = (f32[7,512,128]{2,1,0:T(8,128)}, f32[3,512,128]{2,1,0:T(8,128)}, f32[6,512,128]{2,1,0:T(8,128)}, f32[4,512,128]{2,1,0:T(8,128)}, f32[2,512,128]{2,1,0:T(8,128)}) custom-call(f32[16,128,512]{2,1,0:T(8,128)} %bitcast.12), custom_call_target="tpu_custom_call" | custom-call | flops 1000000000 | bytes 6291456 | tf_op jit(solution)/shard_map/pallas_call | solution.py:94
  22.0 1.3 collective-permute-start.19
  23.5 1.7 collective-permute-start.4
  25.2 3.3 %collective-permute-start.5 = (f32[16,512]{1,0:T(8,128)S(1)}, f32[16,512]{1,0:T(8,128)S(1)}, u32[]{:S(2)}, u32[]{:S(2)}) collective-permute-start(f32[16,512]{1,0:T(8,128)S(1)} %get-tuple-element.40), channel_id=1, source_target_pairs={{0,64},{4,68},{8,72},{12,76},{16,80},{20,84},{24,88},{28,92},{32,9... | collective-permute-start | bytes 98312 | tf_op jit(solution)/shard_map/ppermute | solution.py:397
  31.3 1.4 collective-permute-start.7
  32.7 2.6 %collective-permute-start.8 = (f32[16,512]{1,0:T(8,128)S(1)}, f32[16,512]{1,0:T(8,128)S(1)}, u32[]{:S(2)}, u32[]{:S(2)}) collective-permute-start(f32[16,512]{1,0:T(8,128)S(1)} %add_add_fusion.2), channel_id=1, source_target_pairs={{0,2},{1,3},{2,0},{3,1},{4,6},{5,7},{6,4},{7,5},{8,10},{9,11},{10,... | collective-permute-start | bytes 98312 | tf_op jit(solution)/shard_map/ppermute | solution.py:400
  38.8 3.1 %collective-permute-start.11 = (f32[16,512]{1,0:T(8,128)S(1)}, f32[16,512]{1,0:T(8,128)S(1)}, u32[]{:S(2)}, u32[]{:S(2)}) collective-permute-start(f32[16,512]{1,0:T(8,128)S(1)} %get-tuple-element.28), channel_id=1, source_target_pairs={{0,64},{4,68},{8,72},{12,76},{16,80},{20,84},{24,88},{28,92},{32,9... | collective-permute-start | bytes 98312 | tf_op jit(solution)/shard_map/ppermute | solution.py:401
  42.2 2.7 %shard_map.64 = (f32[6,512,128]{2,1,0:T(8,128)}, f32[4,512,128]{2,1,0:T(8,128)}) custom-call(f32[16,128,512]{2,1,0:T(8,128)} %bitcast.13), custom_call_target="tpu_custom_call" | custom-call | flops 1000000000 | bytes 3145728 | tf_op jit(solution)/shard_map/pallas_call | solution.py:94
  45.0 4.5 %collective-permute-start.17 = (f32[4,512,128]{2,1,0:T(8,128)}, f32[4,512,128]{2,1,0:T(8,128)S(1)}, u32[]{:S(2)}, u32[]{:S(2)}) collective-permute-start(f32[4,512,128]{2,1,0:T(8,128)} %get-tuple-element.21), channel_id=1, source_target_pairs={{0,4},{4,0},{8,12},{12,8},{16,20},{20,16},{24,28},{28,24},{32,36},... | collective-permute-start | bytes 3145736 | tf_op jit(solution)/shard_map/ppermute | solution.py:384
  50.6 2.1 %collective-permute-start.14 = (f32[64,512]{1,0:T(8,128)S(1)}, f32[64,512]{1,0:T(8,128)S(1)}, u32[]{:S(2)}, u32[]{:S(2)}) collective-permute-start(f32[64,512]{1,0:T(8,128)S(1)} %pad_maximum_fusion), channel_id=1, source_target_pairs={{0,16},{4,20},{8,24},{12,28},{16,0},{20,4},{24,8},{28,12},{32,48},... | collective-permute-start | bytes 393224 | tf_op jit(solution)/shard_map/ppermute | solution.py:402
  56.6 1.9 %collective-permute-done.14 = f32[64,512]{1,0:T(8,128)S(1)} collective-permute-done((f32[64,512]{1,0:T(8,128)S(1)}, f32[64,512]{1,0:T(8,128)S(1)}, u32[]{:S(2)}, u32[]{:S(2)}) %collective-permute-start.14) | collective-permute-done | bytes 131104 | tf_op jit(solution)/shard_map/ppermute | solution.py:402
  58.5 1.5 collective-permute-start.18
  61.3 1.8 collective-permute-start.16
  63.4 2.8 %collective-permute-start.23 = (f32[6,512,128]{2,1,0:T(8,128)}, f32[6,512,128]{2,1,0:T(8,128)}, u32[]{:S(2)}, u32[]{:S(2)}) collective-permute-start(f32[6,512,128]{2,1,0:T(8,128)} %get-tuple-element.18.refs_5_), channel_id=1, source_target_pairs={{0,3},{1,0},{2,1},{3,2},{4,7},{5,4},{6,5},{7,6},{8,11},{9,8},{10,9... | collective-permute-start | bytes 4718600 | tf_op jit(solution)/shard_map/ppermute | solution.py:383
  68.0 2.7 %collective-permute-start.30 = (f32[7,512,128]{2,1,0:T(8,128)}, f32[7,512,128]{2,1,0:T(8,128)}, u32[]{:S(2)}, u32[]{:S(2)}) collective-permute-start(f32[7,512,128]{2,1,0:T(8,128)} %get-tuple-element.19.refs_6_), channel_id=1, source_target_pairs={{0,3},{1,0},{2,1},{3,2},{4,7},{5,4},{6,5},{7,6},{8,11},{9,8},{10,9... | collective-permute-start | bytes 5505032 | tf_op jit(solution)/shard_map/ppermute | solution.py:383
  71.8 2.3 %collective-permute-start.21 = (f32[4,512,128]{2,1,0:T(8,128)}, f32[4,512,128]{2,1,0:T(8,128)}, u32[]{:S(2)}, u32[]{:S(2)}) collective-permute-start(f32[4,512,128]{2,1,0:T(8,128)} %copy-done.4), channel_id=1, source_target_pairs={{0,8},{4,124},{8,16},{12,4},{16,24},{20,12},{24,32},{28,20},{32,40... | collective-permute-start | bytes 3145736 | tf_op jit(solution)/shard_map/ppermute | solution.py:385
  74.5 22.0 %collective-permute-done.22.refs_13_ = f32[6,512,128]{2,1,0:T(8,128)} collective-permute-done((f32[6,512,128]{2,1,0:T(8,128)}, f32[6,512,128]{2,1,0:T(8,128)}, u32[]{:S(2)}, u32[]{:S(2)}) %collective-permute-start.22) | collective-permute-done | bytes 1572896 | tf_op jit(solution)/shard_map/ppermute | solution.py:382
  96.5 1.3 collective-permute-start.28
  100.3 2.3 %collective-permute-start.24 = (f32[4,512,128]{2,1,0:T(8,128)}, f32[4,512,128]{2,1,0:T(8,128)S(1)}, u32[]{:S(2)}, u32[]{:S(2)}) collective-permute-start(f32[4,512,128]{2,1,0:T(8,128)} %collective-permute-done.19.refs_10_), channel_id=1, source_target_pairs={{0,8},{4,124},{8,16},{12,4},{16,24},{20,12},{24,32},{28,20},{32,40... | collective-permute-start | bytes 3145736 | tf_op jit(solution)/shard_map/ppermute | solution.py:385
  102.6 33.1 %collective-permute-done.29.refs_2_ = f32[7,512,128]{2,1,0:T(8,128)S(1)} collective-permute-done((f32[7,512,128]{2,1,0:T(8,128)}, f32[7,512,128]{2,1,0:T(8,128)S(1)}, u32[]{:S(2)}, u32[]{:S(2)}) %collective-permute-start.29) | collective-permute-done | bytes 1835040 | tf_op jit(solution)/shard_map/ppermute | solution.py:382
  135.7 3.9 %collective-permute-done.30.refs_3_ = f32[7,512,128]{2,1,0:T(8,128)} collective-permute-done((f32[7,512,128]{2,1,0:T(8,128)}, f32[7,512,128]{2,1,0:T(8,128)}, u32[]{:S(2)}, u32[]{:S(2)}) %collective-permute-start.30) | collective-permute-done | bytes 1835040 | tf_op jit(solution)/shard_map/ppermute | solution.py:383
  139.6 3.4 %collective-permute-start.27 = (f32[3,512,128]{2,1,0:T(8,128)}, f32[3,512,128]{2,1,0:T(8,128)S(1)}, u32[]{:S(2)}, u32[]{:S(2)}) collective-permute-start(f32[3,512,128]{2,1,0:T(8,128)} %get-tuple-element.20.refs_7_), channel_id=1, source_target_pairs={{0,3},{1,0},{2,1},{3,2},{4,7},{5,4},{6,5},{7,6},{8,11},{9,8},{10,9... | collective-permute-start | bytes 2359304 | tf_op jit(solution)/shard_map/ppermute | solution.py:383
  143.0 2.3 %collective-permute-start.25 = (f32[2,512,128]{2,1,0:T(8,128)}, f32[2,512,128]{2,1,0:T(8,128)S(1)}, u32[]{:S(2)}, u32[]{:S(2)}) collective-permute-start(f32[2,512,128]{2,1,0:T(8,128)} %copy-done.7), channel_id=1, source_target_pairs={{0,8},{4,124},{8,16},{12,4},{16,24},{20,12},{24,32},{28,20},{32,40... | collective-permute-start | bytes 1572872 | tf_op jit(solution)/shard_map/ppermute | solution.py:385
  145.3 1.5 copy-done.2
  151.3 19.2 %shard_map.66 = (f32[192,128,128]{2,1,0:T(8,128)}, bf16[16,256,512]{2,1,0:T(8,128)(2,1)S(1)}) custom-call(s32[11]{0:T(128)S(1)} %pad_add_fusion.bounds, s32[264]{0:T(512)S(1)} %broadcast_add_fusion.keys, s32[3]{0:T(128)S(1)} %copy-done.1, f32[16,128,512]{2,1,0:T(8,128)} %bitcast.14, f32[256,512]{1,0:T(8,128)} %constant_dynamic-update-slice_fusion.refs_2_, ...), custom_call_target="tpu_custom_call" | custom-call | flops 6442450944 | bytes 8388608 | tf_op jit(solution)/shard_map/pallas_call | solution.py:343
  170.5 9.2 %shard_map.67.refs_5_ = f32[192,128,128]{2,1,0:T(8,128)} custom-call(s32[11]{0:T(128)S(1)} %pad_add_fusion.bounds, s32[264]{0:T(512)S(1)} %broadcast_add_fusion.keys, bf16[16,256,512]{2,1,0:T(8,128)(2,1)S(1)} %get-tuple-element.25.refs_0_, f32[6,512,128]{2,1,0:T(8,128)} %collective-permute-done.28.refs_1_, ...), custom_call_target="tpu_custom_call", output_to_operand_aliasing={{}: (6, {})} | custom-call | flops 2684354560 | bytes 8388608 | tf_op jit(solution)/shard_map/pallas_call | solution.py:343
  179.7 5.6 %shard_map.68 = f32[192,128,128]{2,1,0:T(8,128)} custom-call(s32[11]{0:T(128)S(1)} %pad_add_fusion.bounds, s32[264]{0:T(512)S(1)} %broadcast_add_fusion.keys, bf16[16,256,512]{2,1,0:T(8,128)(2,1)S(1)} %get-tuple-element.25.refs_0_, f32[4,512,128]{2,1,0:T(8,128)S(1)} %collective-permute-done.24.refs_1_, ...), custom_call_target="tpu_custom_call", output_to_operand_aliasing={{}: (7, {})} | custom-call | flops 1610612736 | bytes 8388608 | tf_op jit(solution)/shard_map/pallas_call | solution.py:343
  (102 shorter events, 26.6 us)
Async XLA Ops:
  8.3 3.2 %collective-permute-start = (f32[256,512]{1,0:T(8,128)}, f32[256,512]{1,0:T(8,128)S(1)}, u32[]{:S(2)}, u32[]{:S(2)}) collective-permute-start(f32[256,512]{1,0:T(8,128)} %get-tuple-element.17), channel_id=1, source_target_pairs={{0,4},{4,0},{8,12},{12,8},{16,20},{20,16},{24,28},{28,24},{32,36},... | collective-permute-start | bytes 1572872 | tf_op jit(solution)/shard_map/ppermute | solution.py:388
  12.7 10.7 %collective-permute-start.1 = (f32[64,512]{1,0:T(8,128)S(1)}, f32[64,512]{1,0:T(8,128)S(1)}, u32[]{:S(2)}, u32[]{:S(2)}) collective-permute-start(f32[64,512]{1,0:T(8,128)S(1)} %get-tuple-element.35), channel_id=1, source_target_pairs={{0,8},{4,12},{8,16},{12,20},{16,24},{20,28},{24,0},{28,4},{32,40},... | collective-permute-start | bytes 393224 | tf_op jit(solution)/shard_map/ppermute | solution.py:392
  14.1 9.3 %collective-permute-start.2 = (f32[64,512]{1,0:T(8,128)S(1)}, f32[64,512]{1,0:T(8,128)S(1)}, u32[]{:S(2)}, u32[]{:S(2)}) collective-permute-start(f32[64,512]{1,0:T(8,128)S(1)} %get-tuple-element.37), channel_id=1, source_target_pairs={{0,16},{4,20},{8,24},{12,28},{16,0},{20,4},{24,8},{28,12},{32,48},... | collective-permute-start | bytes 393224 | tf_op jit(solution)/shard_map/ppermute | solution.py:392
  16.6 6.9 %collective-permute-start.3 = (f32[64,512]{1,0:T(8,128)S(1)}, f32[64,512]{1,0:T(8,128)S(1)}, u32[]{:S(2)}, u32[]{:S(2)}) collective-permute-start(f32[64,512]{1,0:T(8,128)S(1)} %get-tuple-element.36), channel_id=1, source_target_pairs={{0,24},{4,28},{8,0},{12,4},{16,8},{20,12},{24,16},{28,20},{32,56},... | collective-permute-start | bytes 393224 | tf_op jit(solution)/shard_map/ppermute | solution.py:392
  22.0 41.3 %collective-permute-start.19 = (f32[4,512,128]{2,1,0:T(8,128)}, f32[4,512,128]{2,1,0:T(8,128)}, u32[]{:S(2)}, u32[]{:S(2)}) collective-permute-start(f32[4,512,128]{2,1,0:T(8,128)} %get-tuple-element.23), channel_id=1, source_target_pairs={{0,4},{4,0},{8,12},{12,8},{16,20},{20,16},{24,28},{28,24},{32,36},... | collective-permute-start | bytes 3145736 | tf_op jit(solution)/shard_map/ppermute | solution.py:384
  23.3 38.0 %collective-permute-start.20 = (f32[2,512,128]{2,1,0:T(8,128)}, f32[2,512,128]{2,1,0:T(8,128)S(1)}, u32[]{:S(2)}, u32[]{:S(2)}) collective-permute-start(f32[2,512,128]{2,1,0:T(8,128)} %get-tuple-element.24), channel_id=1, source_target_pairs={{0,4},{4,0},{8,12},{12,8},{16,20},{20,16},{24,28},{28,24},{32,36},... | collective-permute-start | bytes 1572872 | tf_op jit(solution)/shard_map/ppermute | solution.py:384
  23.5 5.7 %collective-permute-start.4 = (f32[16,512]{1,0:T(8,128)S(1)}, f32[16,512]{1,0:T(8,128)S(1)}, u32[]{:S(2)}, u32[]{:S(2)}) collective-permute-start(f32[16,512]{1,0:T(8,128)S(1)} %get-tuple-element.38), channel_id=1, source_target_pairs={{0,32},{4,36},{8,40},{12,44},{16,48},{20,52},{24,56},{28,60},{32,6... | collective-permute-start | bytes 98312 | tf_op jit(solution)/shard_map/ppermute | solution.py:397
  25.2 4.9 %collective-permute-start.5 = (f32[16,512]{1,0:T(8,128)S(1)}, f32[16,512]{1,0:T(8,128)S(1)}, u32[]{:S(2)}, u32[]{:S(2)}) collective-permute-start(f32[16,512]{1,0:T(8,128)S(1)} %get-tuple-element.40), channel_id=1, source_target_pairs={{0,64},{4,68},{8,72},{12,76},{16,80},{20,84},{24,88},{28,92},{32,9... | collective-permute-start | bytes 98312 | tf_op jit(solution)/shard_map/ppermute | solution.py:397
  28.5 2.8 %collective-permute-start.6 = (f32[16,512]{1,0:T(8,128)S(1)}, f32[16,512]{1,0:T(8,128)S(1)}, u32[]{:S(2)}, u32[]{:S(2)}) collective-permute-start(f32[16,512]{1,0:T(8,128)S(1)} %get-tuple-element.39), channel_id=1, source_target_pairs={{0,96},{4,100},{8,104},{12,108},{16,112},{20,116},{24,120},{28,124... | collective-permute-start | bytes 98312 | tf_op jit(solution)/shard_map/ppermute | solution.py:397
  31.3 5.1 %collective-permute-start.7 = (f32[16,512]{1,0:T(8,128)S(1)}, f32[16,512]{1,0:T(8,128)S(1)}, u32[]{:S(2)}, u32[]{:S(2)}) collective-permute-start(f32[16,512]{1,0:T(8,128)S(1)} %add_add_fusion.2), channel_id=1, source_target_pairs={{0,1},{1,2},{2,3},{3,0},{4,5},{5,6},{6,7},{7,4},{8,9},{9,10},{10,1... | collective-permute-start | bytes 98312 | tf_op jit(solution)/shard_map/ppermute | solution.py:400
  32.7 4.3 %collective-permute-start.8 = (f32[16,512]{1,0:T(8,128)S(1)}, f32[16,512]{1,0:T(8,128)S(1)}, u32[]{:S(2)}, u32[]{:S(2)}) collective-permute-start(f32[16,512]{1,0:T(8,128)S(1)} %add_add_fusion.2), channel_id=1, source_target_pairs={{0,2},{1,3},{2,0},{3,1},{4,6},{5,7},{6,4},{7,5},{8,10},{9,11},{10,... | collective-permute-start | bytes 98312 | tf_op jit(solution)/shard_map/ppermute | solution.py:400
  35.3 2.9 %collective-permute-start.9 = (f32[16,512]{1,0:T(8,128)S(1)}, f32[16,512]{1,0:T(8,128)S(1)}, u32[]{:S(2)}, u32[]{:S(2)}) collective-permute-start(f32[16,512]{1,0:T(8,128)S(1)} %add_add_fusion.2), channel_id=1, source_target_pairs={{0,3},{1,0},{2,1},{3,2},{4,7},{5,4},{6,5},{7,6},{8,11},{9,8},{10,9... | collective-permute-start | bytes 98312 | tf_op jit(solution)/shard_map/ppermute | solution.py:400
  38.8 6.2 %collective-permute-start.10 = (f32[16,512]{1,0:T(8,128)S(1)}, f32[16,512]{1,0:T(8,128)S(1)}, u32[]{:S(2)}, u32[]{:S(2)}) collective-permute-start(f32[16,512]{1,0:T(8,128)S(1)} %get-tuple-element.28), channel_id=1, source_target_pairs={{0,32},{4,36},{8,40},{12,44},{16,48},{20,52},{24,56},{28,60},{32,6... | collective-permute-start | bytes 98312 | tf_op jit(solution)/shard_map/ppermute | solution.py:401
  38.8 10.6 %collective-permute-start.11 = (f32[16,512]{1,0:T(8,128)S(1)}, f32[16,512]{1,0:T(8,128)S(1)}, u32[]{:S(2)}, u32[]{:S(2)}) collective-permute-start(f32[16,512]{1,0:T(8,128)S(1)} %get-tuple-element.28), channel_id=1, source_target_pairs={{0,64},{4,68},{8,72},{12,76},{16,80},{20,84},{24,88},{28,92},{32,9... | collective-permute-start | bytes 98312 | tf_op jit(solution)/shard_map/ppermute | solution.py:401
  42.0 7.5 %collective-permute-start.12 = (f32[16,512]{1,0:T(8,128)S(1)}, f32[16,512]{1,0:T(8,128)S(1)}, u32[]{:S(2)}, u32[]{:S(2)}) collective-permute-start(f32[16,512]{1,0:T(8,128)S(1)} %get-tuple-element.28), channel_id=1, source_target_pairs={{0,96},{4,100},{8,104},{12,108},{16,112},{20,116},{24,120},{28,124... | collective-permute-start | bytes 98312 | tf_op jit(solution)/shard_map/ppermute | solution.py:401
  45.0 100.4 %copy-start.1 = (s32[3]{0:T(128)S(1)}, s32[3]{0:T(128)}, u32[]{:S(2)}) copy-start(s32[3]{0:T(128)} %pad_add_fusion.1.place.refs_0_) | copy-start | bytes 40
  45.0 21.2 %collective-permute-start.17 = (f32[4,512,128]{2,1,0:T(8,128)}, f32[4,512,128]{2,1,0:T(8,128)S(1)}, u32[]{:S(2)}, u32[]{:S(2)}) collective-permute-start(f32[4,512,128]{2,1,0:T(8,128)} %get-tuple-element.21), channel_id=1, source_target_pairs={{0,4},{4,0},{8,12},{12,8},{16,20},{20,16},{24,28},{28,24},{32,36},... | collective-permute-start | bytes 3145736 | tf_op jit(solution)/shard_map/ppermute | solution.py:384
  49.5 5.7 %collective-permute-start.13 = (f32[64,512]{1,0:T(8,128)S(1)}, f32[64,512]{1,0:T(8,128)S(1)}, u32[]{:S(2)}, u32[]{:S(2)}) collective-permute-start(f32[64,512]{1,0:T(8,128)S(1)} %pad_maximum_fusion), channel_id=1, source_target_pairs={{0,8},{4,12},{8,16},{12,20},{16,24},{20,28},{24,0},{28,4},{32,40},... | collective-permute-start | bytes 393224 | tf_op jit(solution)/shard_map/ppermute | solution.py:402
  50.6 7.9 %collective-permute-start.14 = (f32[64,512]{1,0:T(8,128)S(1)}, f32[64,512]{1,0:T(8,128)S(1)}, u32[]{:S(2)}, u32[]{:S(2)}) collective-permute-start(f32[64,512]{1,0:T(8,128)S(1)} %pad_maximum_fusion), channel_id=1, source_target_pairs={{0,16},{4,20},{8,24},{12,28},{16,0},{20,4},{24,8},{28,12},{32,48},... | collective-permute-start | bytes 393224 | tf_op jit(solution)/shard_map/ppermute | solution.py:402
  55.2 5.4 %collective-permute-start.15 = (f32[64,512]{1,0:T(8,128)S(1)}, f32[64,512]{1,0:T(8,128)S(1)}, u32[]{:S(2)}, u32[]{:S(2)}) collective-permute-start(f32[64,512]{1,0:T(8,128)S(1)} %pad_maximum_fusion), channel_id=1, source_target_pairs={{0,24},{4,28},{8,0},{12,4},{16,8},{20,12},{24,16},{28,20},{32,56},... | collective-permute-start | bytes 393224 | tf_op jit(solution)/shard_map/ppermute | solution.py:402
  58.5 13.3 %collective-permute-start.18 = (f32[6,512,128]{2,1,0:T(8,128)}, f32[6,512,128]{2,1,0:T(8,128)}, u32[]{:S(2)}, u32[]{:S(2)}) collective-permute-start(f32[6,512,128]{2,1,0:T(8,128)} %get-tuple-element.22), channel_id=1, source_target_pairs={{0,4},{4,0},{8,12},{12,8},{16,20},{20,16},{24,28},{28,24},{32,36},... | collective-permute-start | bytes 4718600 | tf_op jit(solution)/shard_map/ppermute | solution.py:384
  60.6 35.9 %collective-permute-start.22 = (f32[6,512,128]{2,1,0:T(8,128)}, f32[6,512,128]{2,1,0:T(8,128)}, u32[]{:S(2)}, u32[]{:S(2)}) collective-permute-start(f32[6,512,128]{2,1,0:T(8,128)} %get-tuple-element.18.refs_5_), channel_id=1, source_target_pairs={{0,1},{1,2},{2,3},{3,0},{4,5},{5,6},{6,7},{7,4},{8,9},{9,10},{10,1... | collective-permute-start | bytes 4718600 | tf_op jit(solution)/shard_map/ppermute | solution.py:382
  61.3 5.9 %collective-permute-start.16 = (f32[256,512]{1,0:T(8,128)}, f32[256,512]{1,0:T(8,128)S(1)}, u32[]{:S(2)}, u32[]{:S(2)}) collective-permute-start(f32[256,512]{1,0:T(8,128)} %constant_dynamic-update-slice_fusion.refs_2_), channel_id=1, source_target_pairs={{0,4},{4,0},{8,12},{12,8},{16,20},{20,16},{24,28},{28,24},{32,36},... | collective-permute-start | bytes 1572872 | tf_op jit(solution)/shard_map/ppermute | solution.py:403
  63.4 36.9 %collective-permute-start.23 = (f32[6,512,128]{2,1,0:T(8,128)}, f32[6,512,128]{2,1,0:T(8,128)}, u32[]{:S(2)}, u32[]{:S(2)}) collective-permute-start(f32[6,512,128]{2,1,0:T(8,128)} %get-tuple-element.18.refs_5_), channel_id=1, source_target_pairs={{0,3},{1,0},{2,1},{3,2},{4,7},{5,4},{6,5},{7,6},{8,11},{9,8},{10,9... | collective-permute-start | bytes 4718600 | tf_op jit(solution)/shard_map/ppermute | solution.py:383
  67.2 68.5 %collective-permute-start.29 = (f32[7,512,128]{2,1,0:T(8,128)}, f32[7,512,128]{2,1,0:T(8,128)S(1)}, u32[]{:S(2)}, u32[]{:S(2)}) collective-permute-start(f32[7,512,128]{2,1,0:T(8,128)} %get-tuple-element.19.refs_6_), channel_id=1, source_target_pairs={{0,1},{1,2},{2,3},{3,0},{4,5},{5,6},{6,7},{7,4},{8,9},{9,10},{10,1... | collective-permute-start | bytes 5505032 | tf_op jit(solution)/shard_map/ppermute | solution.py:382
  68.0 71.6 %collective-permute-start.30 = (f32[7,512,128]{2,1,0:T(8,128)}, f32[7,512,128]{2,1,0:T(8,128)}, u32[]{:S(2)}, u32[]{:S(2)}) collective-permute-start(f32[7,512,128]{2,1,0:T(8,128)} %get-tuple-element.19.refs_6_), channel_id=1, source_target_pairs={{0,3},{1,0},{2,1},{3,2},{4,7},{5,4},{6,5},{7,6},{8,11},{9,8},{10,9... | collective-permute-start | bytes 5505032 | tf_op jit(solution)/shard_map/ppermute | solution.py:383
  71.8 71.2 %collective-permute-start.21 = (f32[4,512,128]{2,1,0:T(8,128)}, f32[4,512,128]{2,1,0:T(8,128)}, u32[]{:S(2)}, u32[]{:S(2)}) collective-permute-start(f32[4,512,128]{2,1,0:T(8,128)} %copy-done.4), channel_id=1, source_target_pairs={{0,8},{4,124},{8,16},{12,4},{16,24},{20,12},{24,32},{28,20},{32,40... | collective-permute-start | bytes 3145736 | tf_op jit(solution)/shard_map/ppermute | solution.py:385
  96.5 74.0 %collective-permute-start.28 = (f32[6,512,128]{2,1,0:T(8,128)}, f32[6,512,128]{2,1,0:T(8,128)}, u32[]{:S(2)}, u32[]{:S(2)}) collective-permute-start(f32[6,512,128]{2,1,0:T(8,128)} %collective-permute-done.18.refs_9_), channel_id=1, source_target_pairs={{0,8},{4,124},{8,16},{12,4},{16,24},{20,12},{24,32},{28,20},{32,40... | collective-permute-start | bytes 4718600 | tf_op jit(solution)/shard_map/ppermute | solution.py:385
  100.3 79.4 %collective-permute-start.24 = (f32[4,512,128]{2,1,0:T(8,128)}, f32[4,512,128]{2,1,0:T(8,128)S(1)}, u32[]{:S(2)}, u32[]{:S(2)}) collective-permute-start(f32[4,512,128]{2,1,0:T(8,128)} %collective-permute-done.19.refs_10_), channel_id=1, source_target_pairs={{0,8},{4,124},{8,16},{12,4},{16,24},{20,12},{24,32},{28,20},{32,40... | collective-permute-start | bytes 3145736 | tf_op jit(solution)/shard_map/ppermute | solution.py:385
  135.7 44.0 %collective-permute-start.26 = (f32[3,512,128]{2,1,0:T(8,128)}, f32[3,512,128]{2,1,0:T(8,128)S(1)}, u32[]{:S(2)}, u32[]{:S(2)}) collective-permute-start(f32[3,512,128]{2,1,0:T(8,128)} %get-tuple-element.20.refs_7_), channel_id=1, source_target_pairs={{0,1},{1,2},{2,3},{3,0},{4,5},{5,6},{6,7},{7,4},{8,9},{9,10},{10,1... | collective-permute-start | bytes 2359304 | tf_op jit(solution)/shard_map/ppermute | solution.py:382
  139.6 40.1 %collective-permute-start.27 = (f32[3,512,128]{2,1,0:T(8,128)}, f32[3,512,128]{2,1,0:T(8,128)S(1)}, u32[]{:S(2)}, u32[]{:S(2)}) collective-permute-start(f32[3,512,128]{2,1,0:T(8,128)} %get-tuple-element.20.refs_7_), channel_id=1, source_target_pairs={{0,3},{1,0},{2,1},{3,2},{4,7},{5,4},{6,5},{7,6},{8,11},{9,8},{10,9... | collective-permute-start | bytes 2359304 | tf_op jit(solution)/shard_map/ppermute | solution.py:383
  143.0 36.7 %collective-permute-start.25 = (f32[2,512,128]{2,1,0:T(8,128)}, f32[2,512,128]{2,1,0:T(8,128)S(1)}, u32[]{:S(2)}, u32[]{:S(2)}) collective-permute-start(f32[2,512,128]{2,1,0:T(8,128)} %copy-done.7), channel_id=1, source_target_pairs={{0,8},{4,124},{8,16},{12,4},{16,24},{20,12},{24,32},{28,20},{32,40... | collective-permute-start | bytes 1572872 | tf_op jit(solution)/shard_map/ppermute | solution.py:385
  (13 other events, 351.6 us)

commit v3 on v2

--- a/solution.py
+++ b/solution.py
@@ -14,9 +14,10 @@
 N_CORE, N_X, N_Z = 2, 4, 4
 N_ROW, N_SUB = N_CORE * N_X * N_Z, 4
 
-SUB_PIECES = (6, 7, 3)
+SUB_PIECES = (6, 8, 2)
 ROW_PIECES = (4, 6, 4, 2)
-STAGES, UNROLL, STEP = 16, 8, 4
+STAGES, STEP = 32, 4
+UNROLLS = (16, 8, 8)
 WHOLE_VMEM = 62 * 2**20
 SELF, NEAR, FAR, SUB_LOW, SUB_HIGH = range(5)
 
@@ -184,10 +185,12 @@
                 sh[rows, :], sl[rows, :] = split(factor[rows, :] * part_of)
 
 
-def make_adjoints(fetch, q, sh, sl, adjoints, keep):
+def make_adjoints(fetch, q, sh, sl, adjoints, keep, turned):
     def some(n, _):
         for u in range(STEP):
             fetch(n * STEP + u).wait()
+        for u in range(STEP):
+            turned[n * STEP + u] = q[n * STEP + u].T
         highs, lows = zip(*[split(q[n * STEP + u]) for u in range(STEP)])
         tall = STEP * BS
         first = jnp.dot(
@@ -209,9 +212,11 @@
 
 
 def pair_kernel(counts, group, bounds, keys, *refs):
-    n_src, n_blk = len(counts), sum(counts)
+    n_src = len(counts)
+    n_own = 0
     if group == 0:
         place, blocks, mine, other, factor = refs[:5]
+        n_own = blocks.shape[0]
         sources = refs[5 : 5 + n_src]
         out, kept_adjoints, adjoints, fetched, stage, sems, fetch_sems = refs[5 + n_src : 12 + n_src]
         q, sh, sl, q_sems, keep_sems = refs[12 + n_src :]
@@ -230,12 +235,13 @@
         sources = refs[1 : 1 + n_src]
         out, adjoints, fetched, stage, sems, fetch_sems, adjoint_sem = refs[2 + n_src :]
         adjoint_copy = pltpu.make_async_copy(given_adjoints, adjoints, adjoint_sem)
+    n_blk = n_own + sum(counts)
     pieces = [(source, b) for source, count in zip(sources, counts) for b in range(count)]
-    for n, (source, b) in enumerate(pieces):
+    for n, (source, b) in enumerate(pieces, n_own):
         pltpu.make_async_copy(source.at[b], fetched.at[n], fetch_sems.at[n]).start()
     if group == 0:
         weigh(place, mine, other, factor, sh, sl)
-        make_adjoints(fetch, q, sh, sl, adjoints, keep)
+        make_adjoints(fetch, q, sh, sl, adjoints, keep, fetched)
     else:
         adjoint_copy.start()
 
@@ -243,10 +249,11 @@
         pltpu.make_async_copy(sources[0].at[0], fetched.at[n], fetch_sems.at[n]).wait()
         return 0
 
-    lax.fori_loop(0, n_blk, arrive, 0)
+    lax.fori_loop(n_own, n_blk, arrive, 0)
     if group:
         adjoint_copy.wait()
     first, last = bounds[group], bounds[group + 1]
+    unroll = UNROLLS[group]
     origin = bounds[group + 8]
     total = last - first
 
@@ -254,9 +261,9 @@
         return pltpu.make_async_copy(stage.at[slot], out.at[target], sems.at[slot])
 
     def some(step, _):
-        at = step * UNROLL
+        at = step * unroll
         products = []
-        names = [keys[first + at + u] for u in range(UNROLL)]
+        names = [keys[first + at + u] for u in range(unroll)]
         for one, two in zip(names[::2], names[1::2]):
             i = (jnp.maximum(one, 0) >> 4) & 15
             b1 = jnp.maximum((one >> 8) - origin, 0)
@@ -276,7 +283,7 @@
             )
             product = by_high[:BS] + (by_high[BS:] + by_low)
             products += [product[:, :BS], product[:, BS:]]
-        for u in range(UNROLL):
+        for u in range(unroll):
             slot = lax.rem(at + u, STAGES)
             before = keys[jnp.maximum(first + at + u - STAGES, 0)]
 
@@ -292,7 +299,7 @@
 
         return 0
 
-    steps = lax.div(total, UNROLL)
+    steps = lax.div(total, unroll)
     lax.fori_loop(0, steps, some, 0)
     for s in range(STAGES):
         at = total - STAGES + s
@@ -308,9 +315,9 @@
 
 def pair_call(group, bounds, keys, sources, out, shape, adjoints, inputs):
     counts = tuple(s.shape[0] for s in sources)
-    n_blk = sum(counts)
     window = sources[0].shape[1]
     rows = inputs[1].shape[0]
+    n_blk = sum(counts) + (rows if group == 0 else 0)
     smem = pl.BlockSpec(memory_space=pltpu.SMEM)
     vmem = pl.BlockSpec(memory_space=pltpu.VMEM)
     hbm = pl.BlockSpec(memory_space=pltpu.HBM)
@@ -348,7 +355,7 @@
         scratch_shapes=scratch,
         input_output_aliases=aliases,
         compiler_params=pltpu.CompilerParams(
-            vmem_limit_bytes=(32, 18, 14)[group] * 2**20
+            vmem_limit_bytes=(34, 18, 14)[group] * 2**20
         ),
         cost_estimate=pl.CostEstimate(
             flops=flops, bytes_accessed=8 * 2**20, transcendentals=0
@@ -447,14 +454,15 @@
     room = (counts + 1) // 2 * 2
     earlier = (jnp.arange(blk_count)[:, None] > jnp.arange(blk_count)[None, :]).astype(jnp.int32)
     row_start = jnp.sum(earlier[:, :, None] * room[None, :, :], axis=1)
-    sizes = (jnp.sum(room, axis=0) + UNROLL - 1) // UNROLL * UNROLL
+    unrolls = jnp.array(UNROLLS, jnp.int32)
+    sizes = (jnp.sum(room, axis=0) + unrolls - 1) // unrolls * unrolls
     starts = jnp.sum(jnp.where(each[:, None] > each[None, :], sizes[None, :], 0), axis=1)
     table = row_start + starts[None, :]
     place_of = within + jnp.sum(
         jnp.where(group_of[:, :, None] == each, table[:, None, :], 0), axis=2
     )
     key = (position * 256 + i_index * 16 + k_index).reshape(-1)
-    n_places = (blk_count * (n_nbr + n_groups) // UNROLL + n_groups) * UNROLL
+    n_places = blk_count * (n_nbr + n_groups) + sum(UNROLLS)
     places = lax.broadcasted_iota(jnp.int32, (n_places, key.shape[0]), 0)
     found = jnp.where(place_of.reshape(1, -1) == places, key[None, :] + 1, 0)
     keys = jnp.sum(found, axis=1) - 1
@@ -467,7 +475,7 @@
     shape = (blk_count * n_nbr, BS, BS)
     inputs = [place, blocks, total, other, factor]
     for index, group in enumerate(groups):
-        arrays = [g[2] for g in group]
+        arrays = [array for slot_of, _, array in group if slot_of != SELF]
         out, adjoints = pair_call(index, bounds, keys, arrays, out, shape, adjoints, inputs)
     return out.reshape(blk_count, n_nbr, BS, BS)
 

time: 186 us -> 192 us (1.032)
  the two profiles are of different devices: /device:TPU:1 before, /device:TPU:2 now
where the time goes in v3:
time: 192 us; the launch traced here: 191 us
  waiting for transfers between devices  87.2 us (45%)
  Pallas kernels  47.7 us (25%)
  starting transfers between devices  42.2 us (22%)
  local copies, waits for them, and re-layouts  7.09 us (4%)
  other arithmetic  5.92 us (3%)
    ppermute x3, waiting for transfers between devices, body(): sub_high = [lax.ppermute(t, 'sub', ring(N_SUB, -1)) for t in sub_own]  43.9 us
    pallas_call x3, Pallas kernels, pair_call(): pl.pallas_call(functools.partial(pair_kernel, counts, group), out_shape=o...  32.9 us
    ppermute x3, waiting for transfers between devices, body(): sub_low = [lax.ppermute(t, 'sub', ring(N_SUB, 1)) for t in sub_own]  28.7 us
    pallas_call x1, Pallas kernels, local_gram(): pl.pallas_call(gram_kernel, out_shape=[jax.ShapeDtypeStruct((window // N_...  7.68 us
    pallas_call x2, Pallas kernels, turn(): pl.pallas_call(functools.partial(turn_kernel, spans), out_shape=[jax.Shap...  7.06 us
    ppermute x3, starting transfers between devices, body(): lax.ppermute(part(total, (z + s) % N_Z, piece), 'row', row_shift(s, 0))  6.69 us
    ppermute x4, starting transfers between devices, body(): far = [lax.ppermute(t, 'row', PASS_ON) for t in near]  6.03 us
    unnamed x27, local copies, waits for them, and re-layouts  5.95 us
  transfers between devices with their start and end apart: 31, of which 11 were waited for; matrix products, arithmetic and copies ran while one was open for 3% of the time, Pallas kernels for 18%

profile of v3, /device:TPU:2, one launch (start us, length us, event | category | flops | bytes accessed | tf_op | source)
XLA Modules:
  0.0 191.3 jit_solution(1721293271688483368)
XLA Ops:
  0.6 7.7 %gram.1 = (f32[256,512]{1,0:T(8,128)}, f32[256,512]{1,0:T(8,128)}) custom-call(s32[3]{0:T(128)} %pad_add_fusion.1.place.refs_0_, f32[16,128,512]{2,1,0:T(8,128)} %bitcast.11, f32[16,128,512]{2,1,0:T(8,128)} %bitcast.16), custom_call_target="tpu_custom_call" | custom-call | flops 3221225472 | bytes 8388608 | tf_op jit(solution)/shard_map/gram/pallas_call | solution.py:158
  8.5 2.0 %collective-permute-done = f32[256,512]{1,0:T(8,128)S(1)} collective-permute-done((f32[256,512]{1,0:T(8,128)}, f32[256,512]{1,0:T(8,128)S(1)}, u32[]{:S(2)}, u32[]{:S(2)}) %collective-permute-start) | collective-permute-done | bytes 524320 | tf_op jit(solution)/shard_map/ppermute | solution.py:395
  12.4 1.5 collective-permute-start.1
  14.9 2.3 %collective-permute-start.3 = (f32[64,512]{1,0:T(8,128)S(1)}, f32[64,512]{1,0:T(8,128)}, u32[]{:S(2)}, u32[]{:S(2)}) collective-permute-start(f32[64,512]{1,0:T(8,128)S(1)} %get-tuple-element.36), channel_id=1, source_target_pairs={{0,24},{4,28},{8,0},{12,4},{16,8},{20,12},{24,16},{28,20},{32,56},... | collective-permute-start | bytes 393224 | tf_op jit(solution)/shard_map/ppermute | solution.py:399
  17.1 4.3 %shard_map.74 = (f32[8,512,128]{2,1,0:T(8,128)}, f32[2,512,128]{2,1,0:T(8,128)}, f32[6,512,128]{2,1,0:T(8,128)}, f32[4,512,128]{2,1,0:T(8,128)}, f32[2,512,128]{2,1,0:T(8,128)}) custom-call(f32[16,128,512]{2,1,0:T(8,128)} %bitcast.12), custom_call_target="tpu_custom_call" | custom-call | flops 1000000000 | bytes 6291456 | tf_op jit(solution)/shard_map/pallas_call | solution.py:95
  23.8 2.1 %collective-permute-start.4 = (f32[16,512]{1,0:T(8,128)S(1)}, f32[16,512]{1,0:T(8,128)S(1)}, u32[]{:S(2)}, u32[]{:S(2)}) collective-permute-start(f32[16,512]{1,0:T(8,128)S(1)} %get-tuple-element.38), channel_id=1, source_target_pairs={{0,32},{4,36},{8,40},{12,44},{16,48},{20,52},{24,56},{28,60},{32,6... | collective-permute-start | bytes 98312 | tf_op jit(solution)/shard_map/ppermute | solution.py:404
  25.9 3.6 %collective-permute-start.5 = (f32[16,512]{1,0:T(8,128)S(1)}, f32[16,512]{1,0:T(8,128)S(1)}, u32[]{:S(2)}, u32[]{:S(2)}) collective-permute-start(f32[16,512]{1,0:T(8,128)S(1)} %get-tuple-element.40), channel_id=1, source_target_pairs={{0,64},{4,68},{8,72},{12,76},{16,80},{20,84},{24,88},{28,92},{32,9... | collective-permute-start | bytes 98312 | tf_op jit(solution)/shard_map/ppermute | solution.py:404
  30.5 1.2 collective-permute-done.5
  31.7 1.7 collective-permute-done.6
  33.4 1.7 collective-permute-start.7
  35.1 2.9 %collective-permute-start.8 = (f32[16,512]{1,0:T(8,128)S(1)}, f32[16,512]{1,0:T(8,128)S(1)}, u32[]{:S(2)}, u32[]{:S(2)}) collective-permute-start(f32[16,512]{1,0:T(8,128)S(1)} %add_add_fusion.2), channel_id=1, source_target_pairs={{0,2},{1,3},{2,0},{3,1},{4,6},{5,7},{6,4},{7,5},{8,10},{9,11},{10,... | collective-permute-start | bytes 98312 | tf_op jit(solution)/shard_map/ppermute | solution.py:407
  38.0 1.3 collective-permute-start.9
  40.5 1.4 collective-permute-done.9
  42.0 3.7 %collective-permute-start.11 = (f32[16,512]{1,0:T(8,128)S(1)}, f32[16,512]{1,0:T(8,128)S(1)}, u32[]{:S(2)}, u32[]{:S(2)}) collective-permute-start(f32[16,512]{1,0:T(8,128)S(1)} %get-tuple-element.28), channel_id=1, source_target_pairs={{0,64},{4,68},{8,72},{12,76},{16,80},{20,84},{24,88},{28,92},{32,9... | collective-permute-start | bytes 98312 | tf_op jit(solution)/shard_map/ppermute | solution.py:408
  46.1 2.8 %shard_map.73 = (f32[6,512,128]{2,1,0:T(8,128)}, f32[4,512,128]{2,1,0:T(8,128)}) custom-call(f32[16,128,512]{2,1,0:T(8,128)} %bitcast.13), custom_call_target="tpu_custom_call" | custom-call | flops 1000000000 | bytes 3145728 | tf_op jit(solution)/shard_map/pallas_call | solution.py:95
  49.6 1.4 collective-permute-start.13
  50.9 1.7 collective-permute-start.14
  52.6 3.1 %collective-permute-done.13 = f32[64,512]{1,0:T(8,128)S(1)} collective-permute-done((f32[64,512]{1,0:T(8,128)S(1)}, f32[64,512]{1,0:T(8,128)S(1)}, u32[]{:S(2)}, u32[]{:S(2)}) %collective-permute-start.13) | collective-permute-done | bytes 131104 | tf_op jit(solution)/shard_map/ppermute | solution.py:409
  55.7 2.1 %collective-permute-start.15 = (f32[64,512]{1,0:T(8,128)S(1)}, f32[64,512]{1,0:T(8,128)S(1)}, u32[]{:S(2)}, u32[]{:S(2)}) collective-permute-start(f32[64,512]{1,0:T(8,128)S(1)} %pad_maximum_fusion), channel_id=1, source_target_pairs={{0,24},{4,28},{8,0},{12,4},{16,8},{20,12},{24,16},{28,20},{32,56},... | collective-permute-start | bytes 393224 | tf_op jit(solution)/shard_map/ppermute | solution.py:409
  58.0 2.7 %collective-permute-done.15 = f32[64,512]{1,0:T(8,128)S(1)} collective-permute-done((f32[64,512]{1,0:T(8,128)S(1)}, f32[64,512]{1,0:T(8,128)S(1)}, u32[]{:S(2)}, u32[]{:S(2)}) %collective-permute-start.15) | collective-permute-done | bytes 131104 | tf_op jit(solution)/shard_map/ppermute | solution.py:409
  62.0 1.4 collective-permute-start.29
  63.4 2.0 %collective-permute-start.30 = (f32[8,512,128]{2,1,0:T(8,128)}, f32[8,512,128]{2,1,0:T(8,128)}, u32[]{:S(2)}, u32[]{:S(2)}) collective-permute-start(f32[8,512,128]{2,1,0:T(8,128)} %get-tuple-element.25), channel_id=1, source_target_pairs={{0,3},{1,0},{2,1},{3,2},{4,7},{5,4},{6,5},{7,6},{8,11},{9,8},{10,9... | collective-permute-start | bytes 6291464 | tf_op jit(solution)/shard_map/ppermute | solution.py:390
  66.3 1.8 collective-permute-start.23
  70.7 28.7 %collective-permute-done.22.refs_10_ = f32[6,512,128]{2,1,0:T(8,128)} collective-permute-done((f32[6,512,128]{2,1,0:T(8,128)}, f32[6,512,128]{2,1,0:T(8,128)}, u32[]{:S(2)}, u32[]{:S(2)}) %collective-permute-start.22) | collective-permute-done | bytes 1572896 | tf_op jit(solution)/shard_map/ppermute | solution.py:389
  102.0 43.9 %collective-permute-done.23.refs_11_ = f32[6,512,128]{2,1,0:T(8,128)} collective-permute-done((f32[6,512,128]{2,1,0:T(8,128)}, f32[6,512,128]{2,1,0:T(8,128)}, u32[]{:S(2)}, u32[]{:S(2)}) %collective-permute-start.23) | collective-permute-done | bytes 1572896 | tf_op jit(solution)/shard_map/ppermute | solution.py:390
  147.8 1.7 collective-permute-start.26
  149.5 1.5 collective-permute-start.27
  151.1 2.8 %collective-permute-start.25 = (f32[2,512,128]{2,1,0:T(8,128)}, f32[2,512,128]{2,1,0:T(8,128)S(1)}, u32[]{:S(2)}, u32[]{:S(2)}) collective-permute-start(f32[2,512,128]{2,1,0:T(8,128)} %collective-permute-done.20.refs_8_), channel_id=1, source_target_pairs={{0,8},{4,124},{8,16},{12,4},{16,24},{20,12},{24,32},{28,20},{32,40... | collective-permute-start | bytes 1572872 | tf_op jit(solution)/shard_map/ppermute | solution.py:392
  153.9 2.2 %copy-done.1 = f32[2048,512]{1,0:T(8,128)S(1)} copy-done((f32[2048,512]{1,0:T(8,128)S(1)}, f32[2048,512]{1,0:T(8,128)}, u32[]{:S(2)}) %copy-start.1) | copy-done | bytes 4194328
  158.1 18.5 %shard_map.75 = (f32[192,128,128]{2,1,0:T(8,128)}, bf16[16,256,512]{2,1,0:T(8,128)(2,1)S(1)}) custom-call(s32[11]{0:T(128)S(1)} %pad_add_fusion.bounds, s32[272]{0:T(512)S(1)} %broadcast_add_fusion.keys, s32[3]{0:T(128)S(1)} %copy-done.4, f32[16,128,512]{2,1,0:T(8,128)S(1)} %bitcast.14, f32[256,512]{1,0:T(8,128)S(1)} %copy-done.3, f32[256,512]{1,0:T(8,128)S(1)} %copy-done.6, ...), custom_call_target="tpu_custom_call" | custom-call | flops 6442450944 | bytes 8388608 | tf_op jit(solution)/shard_map/pallas_call | solution.py:350
  176.6 9.5 %shard_map.76.refs_5_ = f32[192,128,128]{2,1,0:T(8,128)} custom-call(s32[11]{0:T(128)S(1)} %pad_add_fusion.bounds, s32[272]{0:T(512)S(1)} %broadcast_add_fusion.keys, bf16[16,256,512]{2,1,0:T(8,128)(2,1)S(1)} %get-tuple-element.23.refs_0_, f32[6,512,128]{2,1,0:T(8,128)S(1)} %collective-permute-done.28.refs_1_, ...), custom_call_target="tpu_custom_call", output_to_operand_aliasing={{}: (6, {})} | custom-call | flops 2952790016 | bytes 8388608 | tf_op jit(solution)/shard_map/pallas_call | solution.py:350
  186.2 4.9 %shard_map.77 = f32[192,128,128]{2,1,0:T(8,128)} custom-call(s32[11]{0:T(128)S(1)} %pad_add_fusion.bounds, s32[272]{0:T(512)S(1)} %broadcast_add_fusion.keys, bf16[16,256,512]{2,1,0:T(8,128)(2,1)S(1)} %get-tuple-element.23.refs_0_, f32[4,512,128]{2,1,0:T(8,128)S(1)} %collective-permute-done.24.refs_1_, ...), custom_call_target="tpu_custom_call", output_to_operand_aliasing={{}: (7, {})} | custom-call | flops 1342177280 | bytes 8388608 | tf_op jit(solution)/shard_map/pallas_call | solution.py:350
  (96 shorter events, 20.8 us)
Async XLA Ops:
  8.3 2.2 %collective-permute-start = (f32[256,512]{1,0:T(8,128)}, f32[256,512]{1,0:T(8,128)S(1)}, u32[]{:S(2)}, u32[]{:S(2)}) collective-permute-start(f32[256,512]{1,0:T(8,128)} %get-tuple-element.17), channel_id=1, source_target_pairs={{0,4},{4,0},{8,12},{12,8},{16,20},{20,16},{24,28},{28,24},{32,36},... | collective-permute-start | bytes 1572872 | tf_op jit(solution)/shard_map/ppermute | solution.py:395
  12.4 9.7 %collective-permute-start.1 = (f32[64,512]{1,0:T(8,128)}, f32[64,512]{1,0:T(8,128)S(1)}, u32[]{:S(2)}, u32[]{:S(2)}) collective-permute-start(f32[64,512]{1,0:T(8,128)} %get-tuple-element.35), channel_id=1, source_target_pairs={{0,8},{4,12},{8,16},{12,20},{16,24},{20,28},{24,0},{28,4},{32,40},... | collective-permute-start | bytes 393224 | tf_op jit(solution)/shard_map/ppermute | solution.py:399
  13.8 8.2 %collective-permute-start.2 = (f32[64,512]{1,0:T(8,128)S(1)}, f32[64,512]{1,0:T(8,128)}, u32[]{:S(2)}, u32[]{:S(2)}) collective-permute-start(f32[64,512]{1,0:T(8,128)S(1)} %get-tuple-element.37), channel_id=1, source_target_pairs={{0,16},{4,20},{8,24},{12,28},{16,0},{20,4},{24,8},{28,12},{32,48},... | collective-permute-start | bytes 393224 | tf_op jit(solution)/shard_map/ppermute | solution.py:399
  14.9 7.9 %collective-permute-start.3 = (f32[64,512]{1,0:T(8,128)S(1)}, f32[64,512]{1,0:T(8,128)}, u32[]{:S(2)}, u32[]{:S(2)}) collective-permute-start(f32[64,512]{1,0:T(8,128)S(1)} %get-tuple-element.36), channel_id=1, source_target_pairs={{0,24},{4,28},{8,0},{12,4},{16,8},{20,12},{24,16},{28,20},{32,56},... | collective-permute-start | bytes 393224 | tf_op jit(solution)/shard_map/ppermute | solution.py:399
  21.4 40.6 %collective-permute-start.19 = (f32[4,512,128]{2,1,0:T(8,128)}, f32[4,512,128]{2,1,0:T(8,128)S(1)}, u32[]{:S(2)}, u32[]{:S(2)}) collective-permute-start(f32[4,512,128]{2,1,0:T(8,128)} %get-tuple-element.20), channel_id=1, source_target_pairs={{0,4},{4,0},{8,12},{12,8},{16,20},{20,16},{24,28},{28,24},{32,36},... | collective-permute-start | bytes 3145736 | tf_op jit(solution)/shard_map/ppermute | solution.py:391
  21.5 39.4 %collective-permute-start.20 = (f32[2,512,128]{2,1,0:T(8,128)}, f32[2,512,128]{2,1,0:T(8,128)}, u32[]{:S(2)}, u32[]{:S(2)}) collective-permute-start(f32[2,512,128]{2,1,0:T(8,128)} %get-tuple-element.21), channel_id=1, source_target_pairs={{0,4},{4,0},{8,12},{12,8},{16,20},{20,16},{24,28},{28,24},{32,36},... | collective-permute-start | bytes 1572872 | tf_op jit(solution)/shard_map/ppermute | solution.py:391
  23.8 6.7 %collective-permute-start.4 = (f32[16,512]{1,0:T(8,128)S(1)}, f32[16,512]{1,0:T(8,128)S(1)}, u32[]{:S(2)}, u32[]{:S(2)}) collective-permute-start(f32[16,512]{1,0:T(8,128)S(1)} %get-tuple-element.38), channel_id=1, source_target_pairs={{0,32},{4,36},{8,40},{12,44},{16,48},{20,52},{24,56},{28,60},{32,6... | collective-permute-start | bytes 98312 | tf_op jit(solution)/shard_map/ppermute | solution.py:404
  25.9 5.8 %collective-permute-start.5 = (f32[16,512]{1,0:T(8,128)S(1)}, f32[16,512]{1,0:T(8,128)S(1)}, u32[]{:S(2)}, u32[]{:S(2)}) collective-permute-start(f32[16,512]{1,0:T(8,128)S(1)} %get-tuple-element.40), channel_id=1, source_target_pairs={{0,64},{4,68},{8,72},{12,76},{16,80},{20,84},{24,88},{28,92},{32,9... | collective-permute-start | bytes 98312 | tf_op jit(solution)/shard_map/ppermute | solution.py:404
  29.5 3.9 %collective-permute-start.6 = (f32[16,512]{1,0:T(8,128)S(1)}, f32[16,512]{1,0:T(8,128)S(1)}, u32[]{:S(2)}, u32[]{:S(2)}) collective-permute-start(f32[16,512]{1,0:T(8,128)S(1)} %get-tuple-element.39), channel_id=1, source_target_pairs={{0,96},{4,100},{8,104},{12,108},{16,112},{20,116},{24,120},{28,124... | collective-permute-start | bytes 98312 | tf_op jit(solution)/shard_map/ppermute | solution.py:404
  33.4 6.0 %collective-permute-start.7 = (f32[16,512]{1,0:T(8,128)S(1)}, f32[16,512]{1,0:T(8,128)S(1)}, u32[]{:S(2)}, u32[]{:S(2)}) collective-permute-start(f32[16,512]{1,0:T(8,128)S(1)} %add_add_fusion.2), channel_id=1, source_target_pairs={{0,1},{1,2},{2,3},{3,0},{4,5},{5,6},{6,7},{7,4},{8,9},{9,10},{10,1... | collective-permute-start | bytes 98312 | tf_op jit(solution)/shard_map/ppermute | solution.py:407
  35.1 5.4 %collective-permute-start.8 = (f32[16,512]{1,0:T(8,128)S(1)}, f32[16,512]{1,0:T(8,128)S(1)}, u32[]{:S(2)}, u32[]{:S(2)}) collective-permute-start(f32[16,512]{1,0:T(8,128)S(1)} %add_add_fusion.2), channel_id=1, source_target_pairs={{0,2},{1,3},{2,0},{3,1},{4,6},{5,7},{6,4},{7,5},{8,10},{9,11},{10,... | collective-permute-start | bytes 98312 | tf_op jit(solution)/shard_map/ppermute | solution.py:407
  38.0 3.9 %collective-permute-start.9 = (f32[16,512]{1,0:T(8,128)S(1)}, f32[16,512]{1,0:T(8,128)S(1)}, u32[]{:S(2)}, u32[]{:S(2)}) collective-permute-start(f32[16,512]{1,0:T(8,128)S(1)} %add_add_fusion.2), channel_id=1, source_target_pairs={{0,3},{1,0},{2,1},{3,2},{4,7},{5,4},{6,5},{7,6},{8,11},{9,8},{10,9... | collective-permute-start | bytes 98312 | tf_op jit(solution)/shard_map/ppermute | solution.py:407
  41.9 7.0 %collective-permute-start.10 = (f32[16,512]{1,0:T(8,128)S(1)}, f32[16,512]{1,0:T(8,128)S(1)}, u32[]{:S(2)}, u32[]{:S(2)}) collective-permute-start(f32[16,512]{1,0:T(8,128)S(1)} %get-tuple-element.28), channel_id=1, source_target_pairs={{0,32},{4,36},{8,40},{12,44},{16,48},{20,52},{24,56},{28,60},{32,6... | collective-permute-start | bytes 98312 | tf_op jit(solution)/shard_map/ppermute | solution.py:408
  42.0 7.0 %collective-permute-start.11 = (f32[16,512]{1,0:T(8,128)S(1)}, f32[16,512]{1,0:T(8,128)S(1)}, u32[]{:S(2)}, u32[]{:S(2)}) collective-permute-start(f32[16,512]{1,0:T(8,128)S(1)} %get-tuple-element.28), channel_id=1, source_target_pairs={{0,64},{4,68},{8,72},{12,76},{16,80},{20,84},{24,88},{28,92},{32,9... | collective-permute-start | bytes 98312 | tf_op jit(solution)/shard_map/ppermute | solution.py:408
  45.7 3.9 %collective-permute-start.12 = (f32[16,512]{1,0:T(8,128)S(1)}, f32[16,512]{1,0:T(8,128)S(1)}, u32[]{:S(2)}, u32[]{:S(2)}) collective-permute-start(f32[16,512]{1,0:T(8,128)S(1)} %get-tuple-element.28), channel_id=1, source_target_pairs={{0,96},{4,100},{8,104},{12,108},{16,112},{20,116},{24,120},{28,124... | collective-permute-start | bytes 98312 | tf_op jit(solution)/shard_map/ppermute | solution.py:408
  48.9 104.9 %copy-start.4 = (s32[3]{0:T(128)S(1)}, s32[3]{0:T(128)}, u32[]{:S(2)}) copy-start(s32[3]{0:T(128)} %pad_add_fusion.1.place.refs_0_) | copy-start | bytes 40
  48.9 14.5 %collective-permute-start.17 = (f32[4,512,128]{2,1,0:T(8,128)}, f32[4,512,128]{2,1,0:T(8,128)}, u32[]{:S(2)}, u32[]{:S(2)}) collective-permute-start(f32[4,512,128]{2,1,0:T(8,128)} %get-tuple-element.18), channel_id=1, source_target_pairs={{0,4},{4,0},{8,12},{12,8},{16,20},{20,16},{24,28},{28,24},{32,36},... | collective-permute-start | bytes 3145736 | tf_op jit(solution)/shard_map/ppermute | solution.py:391
  49.6 6.1 %collective-permute-start.13 = (f32[64,512]{1,0:T(8,128)S(1)}, f32[64,512]{1,0:T(8,128)S(1)}, u32[]{:S(2)}, u32[]{:S(2)}) collective-permute-start(f32[64,512]{1,0:T(8,128)S(1)} %pad_maximum_fusion), channel_id=1, source_target_pairs={{0,8},{4,12},{8,16},{12,20},{16,24},{20,28},{24,0},{28,4},{32,40},... | collective-permute-start | bytes 393224 | tf_op jit(solution)/shard_map/ppermute | solution.py:409
  50.9 6.9 %collective-permute-start.14 = (f32[64,512]{1,0:T(8,128)S(1)}, f32[64,512]{1,0:T(8,128)S(1)}, u32[]{:S(2)}, u32[]{:S(2)}) collective-permute-start(f32[64,512]{1,0:T(8,128)S(1)} %pad_maximum_fusion), channel_id=1, source_target_pairs={{0,16},{4,20},{8,24},{12,28},{16,0},{20,4},{24,8},{28,12},{32,48},... | collective-permute-start | bytes 393224 | tf_op jit(solution)/shard_map/ppermute | solution.py:409
  55.7 5.0 %collective-permute-start.15 = (f32[64,512]{1,0:T(8,128)S(1)}, f32[64,512]{1,0:T(8,128)S(1)}, u32[]{:S(2)}, u32[]{:S(2)}) collective-permute-start(f32[64,512]{1,0:T(8,128)S(1)} %pad_maximum_fusion), channel_id=1, source_target_pairs={{0,24},{4,28},{8,0},{12,4},{16,8},{20,12},{24,16},{28,20},{32,56},... | collective-permute-start | bytes 393224 | tf_op jit(solution)/shard_map/ppermute | solution.py:409
  57.9 11.4 %collective-permute-start.18 = (f32[6,512,128]{2,1,0:T(8,128)}, f32[6,512,128]{2,1,0:T(8,128)}, u32[]{:S(2)}, u32[]{:S(2)}) collective-permute-start(f32[6,512,128]{2,1,0:T(8,128)} %get-tuple-element.19), channel_id=1, source_target_pairs={{0,4},{4,0},{8,12},{12,8},{16,20},{20,16},{24,28},{28,24},{32,36},... | collective-permute-start | bytes 4718600 | tf_op jit(solution)/shard_map/ppermute | solution.py:391
  60.7 38.8 %collective-permute-start.22 = (f32[6,512,128]{2,1,0:T(8,128)}, f32[6,512,128]{2,1,0:T(8,128)}, u32[]{:S(2)}, u32[]{:S(2)}) collective-permute-start(f32[6,512,128]{2,1,0:T(8,128)} %get-tuple-element.22), channel_id=1, source_target_pairs={{0,1},{1,2},{2,3},{3,0},{4,5},{5,6},{6,7},{7,4},{8,9},{9,10},{10,1... | collective-permute-start | bytes 4718600 | tf_op jit(solution)/shard_map/ppermute | solution.py:389
  60.9 4.6 %collective-permute-start.16 = (f32[256,512]{1,0:T(8,128)S(1)}, f32[256,512]{1,0:T(8,128)S(1)}, u32[]{:S(2)}, u32[]{:S(2)}) collective-permute-start(f32[256,512]{1,0:T(8,128)S(1)} %constant_dynamic-update-slice_fusion.refs_2_), channel_id=1, source_target_pairs={{0,4},{4,0},{8,12},{12,8},{16,20},{20,16},{24,28},{28,24},{32,36},... | collective-permute-start | bytes 1572872 | tf_op jit(solution)/shard_map/ppermute | solution.py:410
  62.0 87.5 %collective-permute-start.29 = (f32[8,512,128]{2,1,0:T(8,128)}, f32[8,512,128]{2,1,0:T(8,128)}, u32[]{:S(2)}, u32[]{:S(2)}) collective-permute-start(f32[8,512,128]{2,1,0:T(8,128)} %get-tuple-element.25), channel_id=1, source_target_pairs={{0,1},{1,2},{2,3},{3,0},{4,5},{5,6},{6,7},{7,4},{8,9},{9,10},{10,1... | collective-permute-start | bytes 6291464 | tf_op jit(solution)/shard_map/ppermute | solution.py:389
  63.4 87.7 %collective-permute-start.30 = (f32[8,512,128]{2,1,0:T(8,128)}, f32[8,512,128]{2,1,0:T(8,128)}, u32[]{:S(2)}, u32[]{:S(2)}) collective-permute-start(f32[8,512,128]{2,1,0:T(8,128)} %get-tuple-element.25), channel_id=1, source_target_pairs={{0,3},{1,0},{2,1},{3,2},{4,7},{5,4},{6,5},{7,6},{8,11},{9,8},{10,9... | collective-permute-start | bytes 6291464 | tf_op jit(solution)/shard_map/ppermute | solution.py:390
  66.3 79.7 %collective-permute-start.23 = (f32[6,512,128]{2,1,0:T(8,128)}, f32[6,512,128]{2,1,0:T(8,128)}, u32[]{:S(2)}, u32[]{:S(2)}) collective-permute-start(f32[6,512,128]{2,1,0:T(8,128)} %get-tuple-element.22), channel_id=1, source_target_pairs={{0,3},{1,0},{2,1},{3,2},{4,7},{5,4},{6,5},{7,6},{8,11},{9,8},{10,9... | collective-permute-start | bytes 4718600 | tf_op jit(solution)/shard_map/ppermute | solution.py:390
  69.3 78.5 %collective-permute-start.21 = (f32[4,512,128]{2,1,0:T(8,128)}, f32[4,512,128]{2,1,0:T(8,128)}, u32[]{:S(2)}, u32[]{:S(2)}) collective-permute-start(f32[4,512,128]{2,1,0:T(8,128)} %collective-permute-done.17.refs_5_), channel_id=1, source_target_pairs={{0,8},{4,124},{8,16},{12,4},{16,24},{20,12},{24,32},{28,20},{32,40... | collective-permute-start | bytes 3145736 | tf_op jit(solution)/shard_map/ppermute | solution.py:392
  99.5 77.2 %collective-permute-start.28 = (f32[6,512,128]{2,1,0:T(8,128)}, f32[6,512,128]{2,1,0:T(8,128)S(1)}, u32[]{:S(2)}, u32[]{:S(2)}) collective-permute-start(f32[6,512,128]{2,1,0:T(8,128)} %collective-permute-done.18.refs_6_), channel_id=1, source_target_pairs={{0,8},{4,124},{8,16},{12,4},{16,24},{20,12},{24,32},{28,20},{32,40... | collective-permute-start | bytes 4718600 | tf_op jit(solution)/shard_map/ppermute | solution.py:392
  146.0 40.2 %collective-permute-start.24 = (f32[4,512,128]{2,1,0:T(8,128)S(1)}, f32[4,512,128]{2,1,0:T(8,128)S(1)}, u32[]{:S(2)}, u32[]{:S(2)}) collective-permute-start(f32[4,512,128]{2,1,0:T(8,128)S(1)} %collective-permute-done.19.refs_7_), channel_id=1, source_target_pairs={{0,8},{4,124},{8,16},{12,4},{16,24},{20,12},{24,32},{28,20},{32,40... | collective-permute-start | bytes 3145736 | tf_op jit(solution)/shard_map/ppermute | solution.py:392
  147.8 38.4 %collective-permute-start.26 = (f32[2,512,128]{2,1,0:T(8,128)}, f32[2,512,128]{2,1,0:T(8,128)S(1)}, u32[]{:S(2)}, u32[]{:S(2)}) collective-permute-start(f32[2,512,128]{2,1,0:T(8,128)} %get-tuple-element.24), channel_id=1, source_target_pairs={{0,1},{1,2},{2,3},{3,0},{4,5},{5,6},{6,7},{7,4},{8,9},{9,10},{10,1... | collective-permute-start | bytes 1572872 | tf_op jit(solution)/shard_map/ppermute | solution.py:389
  149.5 36.7 %collective-permute-start.27 = (f32[2,512,128]{2,1,0:T(8,128)}, f32[2,512,128]{2,1,0:T(8,128)S(1)}, u32[]{:S(2)}, u32[]{:S(2)}) collective-permute-start(f32[2,512,128]{2,1,0:T(8,128)} %get-tuple-element.24), channel_id=1, source_target_pairs={{0,3},{1,0},{2,1},{3,2},{4,7},{5,4},{6,5},{7,6},{8,11},{9,8},{10,9... | collective-permute-start | bytes 1572872 | tf_op jit(solution)/shard_map/ppermute | solution.py:390
  151.1 35.1 %collective-permute-start.25 = (f32[2,512,128]{2,1,0:T(8,128)}, f32[2,512,128]{2,1,0:T(8,128)S(1)}, u32[]{:S(2)}, u32[]{:S(2)}) collective-permute-start(f32[2,512,128]{2,1,0:T(8,128)} %collective-permute-done.20.refs_8_), channel_id=1, source_target_pairs={{0,8},{4,124},{8,16},{12,4},{16,24},{20,12},{24,32},{28,20},{32,40... | collective-permute-start | bytes 1572872 | tf_op jit(solution)/shard_map/ppermute | solution.py:392
  (10 other events, 315.1 us)
